TPU v7x, 32 devices: a whole 2x2x4 slice. The times are simulated.
32 devices in a mesh: grp: 2 (over x), tok: 8 (over z, y), mdl: 2 (over core).
Axes of the slice: x: 2, y: 2, z: 4, core: 2. Of those that a mesh axis runs over, the one named last changes fastest.
Arguments:
- hidden: bfloat16 [1024, 4096], P(('grp', 'tok'), 'mdl'), parts along dimension 0, may hold values from -3 to 3
- queries: bfloat16 [1024, 16, 128], P(('grp', 'tok'), 'mdl'), parts along dimension 0, may hold values from -8 to 8
- cache: bfloat16 [16, 2048, 4, 2, 128], P(('grp', 'tok'), None, 'mdl'), parts along dimension 0, may hold values from -8 to 8
- cache_lengths: int32 [16], P(('grp', 'tok')), parts along dimension 0, may hold values from 128 to 2048, as said below
- wkv: bfloat16 [4096, 4, 2, 128], P('tok', 'mdl'), may hold values from -0.09375 to 0.09375
- wo: bfloat16 [16, 128, 4096], P('mdl', None, 'tok'), may hold values from -0.5 to 0.5
- attn_gain: bfloat16 [4096], replicated, may hold values from 0.5 to 1.5
- moe_gain: bfloat16 [4096], replicated, may hold values from 0.5 to 1.5
- w_gate: bfloat16 [16, 4096, 1792], P(('tok', 'mdl')), may hold values from -0.09375 to 0.09375
- w_up: bfloat16 [16, 4096, 1792], P(('tok', 'mdl')), may hold values from -0.09375 to 0.09375
- w_down: bfloat16 [16, 1792, 4096], P(('tok', 'mdl')), may hold values from -0.0625 to 0.0625
- expert_ids: int32 [1024, 2], P(('grp', 'tok', 'mdl')), parts along dimension 0, may hold values from 0 to 3, all different within a row; in each aligned block of 32 rows (0 to 31, 32 to 63, ...) at most 18 rows name the same one
- gates: float32 [1024, 2], P(('grp', 'tok', 'mdl')), parts along dimension 0, may hold values from 0.1 to 1
Outputs:
- mixed: bfloat16 [1024, 4096], P(('grp', 'tok', 'mdl')), parts along dimension 0
- fresh_key_value: bfloat16 [1024, 4, 2, 128], P(('grp', 'tok'), 'mdl'), parts along dimension 0
There are 2 independent parts, one for each index of `grp`. A program takes and returns all parts, laid end to end along the dimension named above; an argument that names none is the same for every part. Nothing has to cross between parts.
Inputs may be any that keep to these rules, and one draw needn't show every extreme that they name: `expert_ids`: each token names 2 different experts; in aligned blocks of 32 rows no expert is named by more than 18 rows, a bound that some block reaches. `cache_lengths`: some rollout holds exactly 2048 cached positions.
All inputs are finite; a program needn't handle non-finite values.
Results may differ from a plain program's by a relative error of at most 0.007.
Values may be sent and summed in bfloat16 or wider, within the bound.
A program may use at most 128 MiB of HBM per device.

v0:
```python
import functools
import math

import jax
import jax.numpy as jnp
from jax import lax
from jax.experimental import pallas as pl
from jax.experimental.pallas import tpu as pltpu
from jax.sharding import PartitionSpec as P

EXPERTS = 4
TOPK = 2


eps_norm = 1e-05
rope_base = 1000000.0
mask_fill = -1e30


def rms_scale(values_in, gain):
    values = values_in.astype(jnp.float32)
    meansq = jnp.mean(values * values, axis=-1, keepdims=True)
    return values * lax.rsqrt(meansq + eps_norm) * gain.astype(jnp.float32)


def rotate(key_rows, positions):
    half_dim = key_rows.shape[-1] // 2
    inverse = jnp.exp(
        jnp.arange(half_dim, dtype=jnp.float32) * (-2.0 * math.log(rope_base) / key_rows.shape[-1])
    )
    angle = positions.astype(jnp.float32)[:, None] * inverse[None, :]
    cosine = jnp.cos(angle)[:, None, :]
    sine_vals = jnp.sin(angle)[:, None, :]
    front_half = key_rows[..., :half_dim]
    back_half = key_rows[..., half_dim:]
    return jnp.concatenate(
        [front_half * cosine - back_half * sine_vals, back_half * cosine + front_half * sine_vals],
        axis=-1,
    )


def score_rows(query_rows, key_rows, scale_factor):
    return (
        lax.dot_general(
            query_rows, key_rows, (((1,), (1,)), ((), ())), preferred_element_type=jnp.float32
        )
        * scale_factor
    )


MESH = pl.DeviceIdType.MESH
VMEM = pl.BlockSpec(memory_space=pltpu.VMEM)


def place(tok, mdl):
    return (lax.axis_index("grp"), tok, mdl)


def greet(peers):
    barrier = pltpu.get_barrier_semaphore()
    for peer in peers:
        pl.semaphore_signal(barrier, inc=1, device_id=peer, device_id_type=MESH)
    pl.semaphore_wait(barrier, len(peers))


def peers_of(groups, ranks, cores):
    tok, mdl = lax.axis_index("tok"), lax.axis_index("mdl")
    group, rank = tok // ranks, tok % ranks
    peers = [place((group + d) % groups * ranks + rank, mdl) for d in range(1, groups)]
    peers += [place(group * ranks + (rank + d) % ranks, mdl) for d in range(1, ranks)]
    if cores:
        peers.append(place(tok, 1 - mdl))
    return peers


def remote(src, dst, sems, index, device):
    copy = pltpu.make_async_remote_copy(
        src_ref=src,
        dst_ref=dst,
        send_sem=sems.at[0, index],
        recv_sem=sems.at[1, index],
        device_id=device,
        device_id_type=MESH,
    )
    copy.start()
    return copy


def near_first(count):
    return sorted(range(1, count), key=lambda d: (min(d, count - d), d))


def cut(width, pieces):
    part = width // pieces
    return [pl.ds(c * part, part) for c in range(pieces)]


def spread_kernel(groups, ranks, cores, same, pieces, send, out, sems, local_sem):
    tok, mdl = lax.axis_index("tok"), lax.axis_index("mdl")
    group, rank = tok // ranks, tok % ranks
    columns = cut(send.shape[-1], pieces)
    greet(peers_of(groups, ranks, cores))

    def piece(index, c):
        return send.at[:, columns[c]] if same else send.at[index, :, columns[c]]

    def slot(index, c):
        return out.at[index, mdl, :, columns[c]] if cores else out.at[index, :, columns[c]]

    started = []

    def go(src, dst, device):
        copy = remote(src, dst, sems, len(started), device)
        started.append(copy)
        return copy

    first, second, third = {}, [], []
    for c in range(pieces):
        for d in near_first(groups):
            there = (group + d) % groups
            first[c, d] = go(piece(there, c), slot(tok, c), place(there * ranks + rank, mdl))

    def onward(src, index, c):
        for d in near_first(ranks):
            there = group * ranks + (rank + d) % ranks
            second.append((d, index, c, go(src, slot(index, c), place(there, mdl))))

    def across(src, index, c):
        if cores:
            third.append(go(src, slot(index, c), place(tok, 1 - mdl)))

    for c in range(pieces):
        onward(piece(group, c), tok, c)
    for c in range(pieces):
        across(piece(group, c), tok, c)
    own = pltpu.make_async_copy(
        send if same else send.at[group], out.at[tok, mdl] if cores else out.at[tok], local_sem
    )
    own.start()
    for c in range(pieces):
        for d in near_first(groups):
            first[c, d].wait_recv()
            index = (group + groups - d) % groups * ranks + rank
            onward(slot(index, c), index, c)
            across(slot(index, c), index, c)
    for d, index, c, copy in second:
        copy.wait_recv()
        index = index // ranks * ranks + (rank + ranks - d) % ranks
        across(slot(index, c), index, c)
    for copy in third:
        copy.wait_recv()
    for copy in started:
        copy.wait_send()
    own.wait()


def spread(send, groups, ranks, cores, same, number, pieces=1):
    tiles = send.shape if same else send.shape[1:]
    toks = groups * ranks
    core_count = lax.axis_size("mdl") if cores else 1
    lead = (toks, core_count) if cores else (toks,)
    copies = pieces * (groups - 1 + groups * (ranks - 1) + (toks if cores else 0))
    return pl.pallas_call(
        functools.partial(spread_kernel, groups, ranks, cores, same, pieces),
        out_shape=jax.ShapeDtypeStruct(lead + tiles, send.dtype),
        in_specs=[VMEM],
        out_specs=VMEM,
        scratch_shapes=[pltpu.SemaphoreType.DMA((2, copies)), pltpu.SemaphoreType.DMA],
        compiler_params=pltpu.CompilerParams(
            collective_id=number, has_side_effects=True, vmem_limit_bytes=40 * 1024 * 1024
        ),
    )(send)


def collect_kernel(groups, ranks, pieces, parts, out, near, held, mid, sems):
    tok, mdl = lax.axis_index("tok"), lax.axis_index("mdl")
    group, rank = tok // ranks, tok % ranks
    columns = cut(parts.shape[-1], pieces)
    greet(peers_of(groups, ranks, True))
    started = []

    def go(src, dst, device):
        copy = remote(src, dst, sems, len(started), device)
        started.append(copy)
        return copy

    far = near_first(groups)[::-1] + [0]
    order = [(r, g) for r in near_first(ranks) + [0] for g in far]

    def index_of(r, g):
        return (group + g) % groups * ranks + (rank + r) % ranks

    across, second, last = {}, {}, []
    for c in range(pieces):
        for r, g in order:
            index = index_of(r, g)
            across[c, r, g] = go(
                parts.at[index, 1 - mdl, :, columns[c]],
                near.at[index, :, columns[c]],
                place(tok, 1 - mdl),
            )

    def both_cores(c, r, g):
        index = index_of(r, g)
        across[c, r, g].wait_recv()
        return parts[index, mdl, :, columns[c]].astype(jnp.float32) + near[
            index, :, columns[c]
        ].astype(jnp.float32)

    def to_ranks(c):
        for r, g in order:
            if r == 0:
                continue
            index = index_of(r, g)
            held[index, :, columns[c]] = both_cores(c, r, g).astype(held.dtype)
            second[c, r, g] = go(
                held.at[index, :, columns[c]],
                mid.at[r - 1, g, :, columns[c]],
                place(group * ranks + (rank + r) % ranks, mdl),
            )

    def to_sources(c):
        for g in far:
            index = index_of(0, g)
            total = both_cores(c, 0, g)
            for r in range(1, ranks):
                second[c, r, g].wait_recv()
                total = total + mid[r - 1, g, :, columns[c]].astype(jnp.float32)
            if g == 0:
                out[group, :, columns[c]] = total.astype(out.dtype)
            else:
                held[index, :, columns[c]] = total.astype(held.dtype)
                last.append(
                    go(
                        held.at[index, :, columns[c]],
                        out.at[group, :, columns[c]],
                        place((group + g) % groups * ranks + rank, mdl),
                    )
                )

    for c in range(pieces + 1):
        if c < pieces:
            to_ranks(c)
        if c > 0:
            to_sources(c - 1)
    for copy in last:
        copy.wait_recv()
    for copy in started:
        copy.wait_send()


def collect(parts, groups, ranks, number, pieces=1):
    toks = groups * ranks
    tile = parts.shape[2:]
    copies = pieces * (toks + groups * (ranks - 1) + groups - 1)
    return pl.pallas_call(
        functools.partial(collect_kernel, groups, ranks, pieces),
        out_shape=jax.ShapeDtypeStruct((groups,) + tile, parts.dtype),
        in_specs=[VMEM],
        out_specs=VMEM,
        scratch_shapes=[
            pltpu.VMEM((toks,) + tile, parts.dtype),
            pltpu.VMEM((toks,) + tile, parts.dtype),
            pltpu.VMEM((max(ranks - 1, 1), groups) + tile, parts.dtype),
            pltpu.SemaphoreType.DMA((2, copies)),
        ],
        compiler_params=pltpu.CompilerParams(
            collective_id=number, has_side_effects=True, vmem_limit_bytes=40 * 1024 * 1024
        ),
    )(parts)


def attention_kernel(length, queries, cached, fresh, out):
    heads, span, width = queries.shape
    rows = heads * span
    query_rows = queries[...].reshape(rows, width)
    scale_factor = 1.0 / math.sqrt(width)
    limit = cached.shape[2]
    block = min(512, limit)
    token = lax.broadcasted_iota(jnp.int32, (rows, span), 0) % span
    column = lax.broadcasted_iota(jnp.int32, (rows, span), 1)
    scores = [
        jnp.where(
            column <= token, score_rows(query_rows, fresh[0, 0], scale_factor), mask_fill
        )
    ]
    values = [fresh[0, 1]]
    for start in range(0, limit, block):
        position = lax.broadcasted_iota(jnp.int32, (rows, block), 1) + start
        found = score_rows(query_rows, cached[0, 0, pl.ds(start, block)], scale_factor)
        scores.append(jnp.where(position < length[0], found, mask_fill))
        values.append(cached[0, 1, pl.ds(start, block)])
    top = functools.reduce(jnp.maximum, [jnp.max(x, axis=1, keepdims=True) for x in scores])
    total = jnp.zeros((rows, 1), jnp.float32)
    mixed = jnp.zeros((rows, width), jnp.float32)
    for found, value_rows in zip(scores, values):
        weights = jnp.exp(found - top)
        total += jnp.sum(weights, axis=1, keepdims=True)
        mixed += jnp.dot(
            weights.astype(jnp.bfloat16), value_rows, preferred_element_type=jnp.float32
        )
    attended = (mixed / total).astype(out.dtype)
    for head in range(heads):
        out[:, head * width : (head + 1) * width] = attended[head * span : (head + 1) * span]


def attention(queries, cache, lengths, fresh):
    span, query_heads, width = queries.shape
    kv_heads = cache.shape[2]
    per_head = query_heads // kv_heads
    limit = cache.shape[1]
    return pl.pallas_call(
        attention_kernel,
        grid=(kv_heads,),
        out_shape=jax.ShapeDtypeStruct((span, query_heads * width), jnp.bfloat16),
        in_specs=[
            pl.BlockSpec(memory_space=pltpu.SMEM),
            pl.BlockSpec((per_head, span, width), lambda h: (h, 0, 0)),
            pl.BlockSpec((1, 2, limit, width), lambda h: (h, 0, 0, 0)),
            pl.BlockSpec((1, 2, span, width), lambda h: (h, 0, 0, 0)),
        ],
        out_specs=pl.BlockSpec((span, per_head * width), lambda h: (0, h)),
        compiler_params=pltpu.CompilerParams(vmem_limit_bytes=40 * 1024 * 1024),
    )(
        lengths,
        queries.transpose(1, 0, 2),
        cache[0].transpose(1, 2, 0, 3),
        fresh.transpose(1, 2, 0, 3),
    )


def shards(
    hidden,
    queries,
    cache,
    cache_lengths,
    wkv,
    wo,
    attn_gain,
    moe_gain,
    w_gate,
    w_up,
    w_down,
    expert_ids,
    gates,
):
    full_rows = lax.all_gather(hidden, "mdl", axis=1, tiled=True)
    span_len = full_rows.shape[0]
    toks = lax.axis_size("tok")
    core_count = lax.axis_size("mdl")
    ranks = toks // EXPERTS
    core_rows = span_len // core_count
    core_start = lax.axis_index("mdl") * core_rows
    own_rows = lax.dynamic_slice_in_dim(full_rows, core_start, core_rows, 0)
    normalized_input = rms_scale(own_rows, attn_gain).astype(jnp.bfloat16)
    kv_heads = wkv.shape[1]
    head_dim = wkv.shape[3]
    depth = wkv.shape[0]
    slices = normalized_input.reshape(core_rows, toks, depth).transpose(1, 0, 2)
    every_row = spread(slices, toks, 1, True, False, 1).reshape(-1, depth)
    partial_kv = jnp.dot(
        every_row, wkv.reshape(depth, -1), preferred_element_type=jnp.float32
    ).astype(jnp.bfloat16)
    terms = spread(partial_kv.reshape(toks, span_len, -1), toks, 1, False, False, 2)
    key_value_projection = jnp.sum(terms.astype(jnp.float32), axis=0).reshape(
        span_len, kv_heads, 2, head_dim
    )
    length = cache_lengths[0]
    positions = length + jnp.arange(span_len, dtype=jnp.int32)
    fresh_key_value = jnp.stack(
        [rotate(key_value_projection[:, :, 0], positions), key_value_projection[:, :, 1]], axis=2
    ).astype(jnp.bfloat16)
    heads_out = attention(queries, cache, cache_lengths, fresh_key_value)
    every_head = spread(heads_out, EXPERTS, ranks, False, True, 3, 2)
    attn_part = jnp.dot(
        every_head.reshape(toks * span_len, -1),
        wo.reshape(-1, wo.shape[2]),
        preferred_element_type=jnp.float32,
    ).astype(jnp.bfloat16)
    attn_rows = collect(
        attn_part.reshape(toks, core_count, core_rows, -1), toks, 1, 4
    )
    attn_rows = attn_rows.transpose(1, 0, 2).reshape(core_rows, -1).astype(jnp.float32)
    resid = own_rows.astype(jnp.float32) + attn_rows
    moe_in = rms_scale(resid, moe_gain).astype(jnp.bfloat16)
    expert_range = jnp.arange(EXPERTS)
    matches = expert_ids[:, :, None] == expert_range[None, None, :]
    chosen = jnp.sum(matches.astype(jnp.int32), axis=1)
    route = jnp.sum(jnp.where(matches, gates[:, :, None], 0.0), axis=1)
    slot_of = jnp.cumsum(chosen, axis=0) - chosen
    capacity = core_rows * TOPK * 9 // (8 * EXPERTS)
    slot_range = jnp.arange(capacity)
    select = (slot_of.T[:, None, :] == slot_range[None, :, None]) & (chosen.T[:, None, :] > 0)
    send_rows = jnp.einsum(
        "eci,id->ecd", select.astype(jnp.bfloat16), moe_in, preferred_element_type=jnp.float32
    ).astype(jnp.bfloat16)
    model_width = moe_in.shape[1]
    received = spread(send_rows, EXPERTS, ranks, True, False, 5, 4)
    flat_rows = received.reshape(-1, model_width)
    gate_val = jnp.dot(flat_rows, w_gate[0], preferred_element_type=jnp.float32)
    up_val = jnp.dot(flat_rows, w_up[0], preferred_element_type=jnp.float32)
    slab_hidden = (jax.nn.silu(gate_val) * up_val).astype(jnp.bfloat16)
    slab_out = jnp.dot(slab_hidden, w_down[0], preferred_element_type=jnp.float32).astype(
        jnp.bfloat16
    )
    summed = collect(slab_out.reshape(received.shape), EXPERTS, ranks, 6, 4).astype(jnp.float32)
    weight_table = select.astype(jnp.float32) * route.T[:, None, :]
    moe_out = jnp.einsum("eci,ecd->id", weight_table, summed, precision=lax.Precision.HIGHEST)
    mixed = (resid + moe_out).astype(jnp.bfloat16)
    return (mixed, fresh_key_value)


def solution(mesh):
    in_specs = (
        P(("grp", "tok"), "mdl"),
        P(("grp", "tok"), "mdl", None),
        P(("grp", "tok"), None, "mdl", None, None),
        P(("grp", "tok")),
        P("tok", "mdl", None, None),
        P("mdl", None, "tok"),
        P(),
        P(),
        P(("tok", "mdl"), None, None),
        P(("tok", "mdl"), None, None),
        P(("tok", "mdl"), None, None),
        P(("grp", "tok", "mdl"), None),
        P(("grp", "tok", "mdl"), None),
    )
    out_specs = (P(("grp", "tok", "mdl"), None), P(("grp", "tok"), "mdl", None, None))
    return jax.shard_map(shards, mesh=mesh, in_specs=in_specs, out_specs=out_specs, check_vma=False)
```

profile of v0, /device:TPU:0, one launch (start us, length us, event | category | flops | bytes accessed | tf_op | source)
XLA Modules:
  0.0 157.1 jit_solution(15841421066906719680)
XLA Ops:
  0.7 2.6 %all_gather.3 = bf16[64,4096]{1,0:T(8,128)(2,1)S(1)} all-gather(bf16[64,2048]{1,0:T(8,128)(2,1)} %param.13), channel_id=1, replica_groups=mesh['grp'=2,'tok'=8,'mdl'=2] {'mdl'}, dimensions={1}, use_global_device_ids=true | all-gather | bytes 786432 | tf_op jit(solution)/shard_map/all_gather | solution.py:347
  3.3 0.2 fusion.17
  3.5 0.7 convert_element_type.61
  4.2 0.1 fusion.19
  4.4 14.0 %shard_map.140 = bf16[8,2,32,512]{3,2,1,0:T(8,128)(2,1)S(1)} custom-call(bf16[8,32,512]{2,1,0:T(8,128)(2,1)S(1)} %bitcast.74), custom_call_target="tpu_custom_call" | custom-call | tf_op jit(solution)/shard_map/pallas_call | solution.py:163
  18.4 0.2 reshape.120
  18.6 0.4 convolution_convert_fusion.1
  19.0 15.9 %shard_map.141 = bf16[8,64,512]{2,1,0:T(8,128)(2,1)S(1)} custom-call(bf16[8,64,512]{2,1,0:T(8,128)(2,1)S(1)} %bitcast.73), custom_call_target="tpu_custom_call" | custom-call | tf_op jit(solution)/shard_map/pallas_call | solution.py:163
  35.0 0.1 reshape.122
  35.9 0.2 multiply_cosine_fusion
  36.1 0.1 subtract_convert_fusion
  36.2 0.1 maximum_bitcast_fusion
  36.4 1.9 %copy.54 = bf16[1,2048,2,2,128]{4,1,3,2,0:T(8,128)(2,1)S(1)} copy(bf16[1,2048,2,2,128]{4,3,2,1,0:T(2,128)(2,1)} %param.15) | data formatting | bytes 4194304 | tf_op args[2]
  38.3 2.2 %shard_map.142.send = bf16[64,1024]{1,0:T(8,128)(2,1)S(1)} custom-call(s32[1]{0:T(128)} %copy.58.length, bf16[8,64,128]{2,1,0:T(8,128)(2,1)S(1)} %bitcast.77, bf16[2,2,2048,128]{3,2,1,0:T(8,128)(2,1)S(1)} %bitcast.71, bf16[2,2,64,128]{3,2,1,0:T(8,128)(2,1)S(1)} %get-tuple-element.11.fresh), custom_call_target="tpu_custom_call" | custom-call | tf_op jit(solution)/shard_map/pallas_call | solution.py:312
  40.5 18.1 %shard_map.143 = bf16[8,64,1024]{2,1,0:T(8,128)(2,1)S(1)} custom-call(bf16[64,1024]{1,0:T(8,128)(2,1)S(1)} %shard_map.142.send), custom_call_target="tpu_custom_call" | custom-call | tf_op jit(solution)/shard_map/pallas_call | solution.py:163
  58.6 0.7 convolution_convert_fusion.2
  59.3 10.4 %shard_map.144 = bf16[8,32,512]{2,1,0:T(8,128)(2,1)S(1)} custom-call(bf16[8,2,32,512]{3,2,1,0:T(8,128)(2,1)S(1)} %bitcast.76), custom_call_target="tpu_custom_call" | custom-call | tf_op jit(solution)/shard_map/pallas_call | solution.py:256
  69.8 0.2 multiply_reduce_fusion
  70.1 0.1 copy.40
  70.2 0.1 copy.42
  70.3 0.3 copy-done.3
  70.6 0.4 convolution_convert_fusion.send
  71.0 27.9 %shard_map.145 = bf16[8,2,18,4096]{3,2,1,0:T(8,128)(2,1)S(1)} custom-call(bf16[4,18,4096]{2,1,0:T(8,128)(2,1)S(1)} %convolution_convert_fusion.send), custom_call_target="tpu_custom_call" | custom-call | tf_op jit(solution)/shard_map/pallas_call | solution.py:163
  99.0 2.3 %reshape.126 = bf16[288,4096]{1,0:T(8,128)(2,1)} reshape(bf16[8,2,18,4096]{3,2,1,0:T(8,128)(2,1)S(1)} %shard_map.145) | data formatting | bytes 4718592 | tf_op jit(solution)/shard_map/reshape | solution.py:399
  101.3 9.1 %fusion.4 = f32[288,1792]{1,0:T(8,128)S(1)} fusion(bf16[288,4096]{1,0:T(8,128)(2,1)} %reshape.126, bf16[1,4096,1792]{2,1,0:T(8,128)(2,1)} %param.21), kind=kOutput, calls=%fused_computation.4 | convolution fusion | flops 4227858432 | bytes 19103744 | tf_op jit(solution)/shard_map/dot_general | solution.py:400
  110.4 9.9 %fusion.14 = bf16[288,1792]{1,0:T(8,128)(2,1)S(1)} fusion(bf16[288,4096]{1,0:T(8,128)(2,1)S(1)} %copy-done.7, bf16[1,4096,1792]{2,1,0:T(8,128)(2,1)} %param.22, f32[288,1792]{1,0:T(8,128)S(1)} %fusion.4), kind=kOutput, calls=%fused_computation.12 | convolution fusion | flops 4230955008 | bytes 20135936 | tf_op jit(solution)/shard_map/dot_general | solution.py:401
  120.4 4.8 %fusion.6 = bf16[288,4096]{1,0:T(8,128)(2,1)S(1)} fusion(bf16[288,1792]{1,0:T(8,128)(2,1)S(1)} %fusion.14, bf16[1,1792,4096]{2,1,0:T(8,128)(2,1)S(1)} %bitcast.85), kind=kOutput, calls=%fused_computation.6 | convolution fusion | flops 4229038080 | bytes 18071552 | tf_op jit(solution)/shard_map/dot_general | solution.py:403
  125.2 2.4 %reshape.127.parts = bf16[8,2,18,4096]{3,2,1,0:T(8,128)(2,1)} reshape(bf16[288,4096]{1,0:T(8,128)(2,1)S(1)} %fusion.6) | data formatting | bytes 4718592 | tf_op jit(solution)/shard_map/reshape | solution.py:406
  127.6 1.9 %copy-done.2 = bf16[8,2,18,4096]{3,2,1,0:T(8,128)(2,1)S(1)} copy-done((bf16[8,2,18,4096]{3,2,1,0:T(8,128)(2,1)S(1)}, bf16[8,2,18,4096]{3,2,1,0:T(8,128)(2,1)}, u32[]{:S(2)}) %copy-start.2) | copy-done | bytes 2359320
  129.5 25.6 %shard_map.146 = bf16[4,18,4096]{2,1,0:T(8,128)(2,1)S(1)} custom-call(bf16[8,2,18,4096]{3,2,1,0:T(8,128)(2,1)S(1)} %copy-done.2), custom_call_target="tpu_custom_call" | custom-call | tf_op jit(solution)/shard_map/pallas_call | solution.py:256
  155.2 1.2 fusion.10
  156.4 0.7 copy.43
  (53 shorter events, 0.6 us)
Async XLA Ops:
  0.6 58.0 %copy-start = (bf16[8,128,512]{2,1,0:T(8,128)(2,1)S(1)}, bf16[8,128,512]{2,1,0:T(8,128)(2,1)}, u32[]{:S(2)}) copy-start(bf16[8,128,512]{2,1,0:T(8,128)(2,1)} %param.18) | copy-start | bytes 3145732
  0.6 17.7 %copy-start.8 = (bf16[512,2,2,128]{3,2,1,0:T(2,128)(2,1)S(1)}, bf16[512,2,2,128]{3,2,1,0:T(2,128)(2,1)}, u32[]{:S(2)}) copy-start(bf16[512,2,2,128]{3,2,1,0:T(2,128)(2,1)} %param.17) | copy-start | bytes 1572868
  3.3 67.0 %copy-start.5 = (bf16[64,4096]{1,0:T(8,128)(2,1)}, bf16[64,4096]{1,0:T(8,128)(2,1)S(1)}, u32[]{:S(2)}) copy-start(bf16[64,4096]{1,0:T(8,128)(2,1)S(1)} %all_gather.3) | copy-start | bytes 1572868
  36.2 2.1 %copy-start.9 = (bf16[64,8,128]{2,1,0:T(8,128)(2,1)S(1)}, bf16[64,8,128]{2,1,0:T(8,128)(2,1)}, u32[]{:S(2)}) copy-start(bf16[64,8,128]{2,1,0:T(8,128)(2,1)} %param.14) | copy-start | bytes 393220
  59.3 10.7 %copy-start.11 = (s32[32,2]{0,1:T(2,128)S(1)}, s32[32,2]{0,1:T(2,128)}, u32[]{:S(2)}) copy-start(s32[32,2]{0,1:T(2,128)} %param.24) | copy-start | bytes 772
  59.3 11.0 %copy-start.10 = (bf16[4096]{0:T(1024)(128)(2,1)S(1)}, bf16[4096]{0:T(1024)(128)(2,1)}, u32[]{:S(2)}) copy-start(bf16[4096]{0:T(1024)(128)(2,1)} %param.20) | copy-start | bytes 24580
  69.8 0.8 copy-start.3
  101.3 9.1 %copy-start.7 = (bf16[288,4096]{1,0:T(8,128)(2,1)S(1)}, bf16[288,4096]{1,0:T(8,128)(2,1)}, u32[]{:S(2)}) copy-start(bf16[288,4096]{1,0:T(8,128)(2,1)} %reshape.126) | copy-start | bytes 7077892
  101.3 19.0 %slice-start = ((s8[14680064]{0:T(1024)(128)(4,1)}), s8[4194304]{0:T(1024)(128)(4,1)S(1)}, s32[]{:S(2)}) async-start(s8[14680064]{0:T(1024)(128)(4,1)} %bitcast.84), calls=%async_computation | async-start | bytes 8388608
  101.3 19.0 %slice-start.1 = ((s8[14680064]{0:T(1024)(128)(4,1)}), s8[4194304]{0:T(1024)(128)(4,1)S(1)}, s32[]{:S(2)}) async-start(s8[14680064]{0:T(1024)(128)(4,1)} %bitcast.84), calls=%async_computation.1 | async-start | bytes 8388608
  110.4 9.9 %slice-start.2 = ((s8[14680064]{0:T(1024)(128)(4,1)}), s8[4194304]{0:T(1024)(128)(4,1)S(1)}, s32[]{:S(2)}) async-start(s8[14680064]{0:T(1024)(128)(4,1)} %bitcast.84), calls=%async_computation.2 | async-start | bytes 8388608
  110.4 9.9 %slice-start.3 = ((s8[14680064]{0:T(1024)(128)(4,1)}), s8[2097152]{0:T(1024)(128)(4,1)S(1)}, s32[]{:S(2)}) async-start(s8[14680064]{0:T(1024)(128)(4,1)} %bitcast.84), calls=%async_computation.3 | async-start | bytes 4194304
  125.2 31.9 %copy-start.1 = (bf16[8,128,512]{2,1,0:T(8,128)(2,1)S(1)}, bf16[8,128,512]{2,1,0:T(8,128)(2,1)}, u32[]{:S(2)}) copy-start(bf16[8,128,512]{2,1,0:T(8,128)(2,1)} %param.18) | copy-start | bytes 3145732
  127.6 1.9 %copy-start.2 = (bf16[8,2,18,4096]{3,2,1,0:T(8,128)(2,1)S(1)}, bf16[8,2,18,4096]{3,2,1,0:T(8,128)(2,1)}, u32[]{:S(2)}) copy-start(bf16[8,2,18,4096]{3,2,1,0:T(8,128)(2,1)} %reshape.127.parts) | copy-start | bytes 7077892
  129.5 25.6 %copy-start.12 = (f32[32,2]{0,1:T(2,128)S(1)}, f32[32,2]{0,1:T(2,128)}, u32[]{:S(2)}) copy-start(f32[32,2]{0,1:T(2,128)} %param.25) | copy-start | bytes 772
  129.5 25.7 %copy-start.4 = (f32[8,4,8,512]{3,2,0,1:T(8,128)S(1)}, f32[8,4,8,512]{3,2,0,1:T(8,128)}, u32[]{:S(2)}) copy-start(f32[8,4,8,512]{3,2,0,1:T(8,128)} %copy-done.3) | copy-start | bytes 1572868
  129.5 25.7 %copy-start.6 = (bf16[64,4096]{1,0:T(8,128)(2,1)S(1)}, bf16[64,4096]{1,0:T(8,128)(2,1)}, u32[]{:S(2)}) copy-start(bf16[64,4096]{1,0:T(8,128)(2,1)} %copy-done.5) | copy-start | bytes 1572868
where the time goes:
time: 157 us
  Pallas kernels  114 us (73%)
  matrix products  26.6 us (17%)
  local copies, waits for them, and re-layouts  10.2 us (6%)
  blocking collectives  2.64 us (2%)
  other arithmetic  1.84 us (1%)
  between operations  1.72 us (1%)
    pallas_call x4, Pallas kernels, spread(): pl.pallas_call(functools.partial(spread_kernel, groups, ranks, cores, sam...  75.9 us
    pallas_call x2, Pallas kernels, collect(): pl.pallas_call(functools.partial(collect_kernel, groups, ranks, pieces),...  36 us
    dot_general x1, matrix products, shards(): up_val = jnp.dot(flat_rows, w_up[0], preferred_element_type=jnp.float32)  9.85 us
    dot_general x1, matrix products, shards(): gate_val = jnp.dot(flat_rows, w_gate[0], preferred_element_type=jnp.float32)  9.13 us
    unnamed x39, local copies, waits for them, and re-layouts  4.86 us
    dot_general x1, matrix products, shards(): jnp.dot(slab_hidden, w_down[0], preferred_element_type=jnp.float32)  4.82 us

commit v1 on v0

--- a/solution.py
+++ b/solution.py
@@ -1,4 +1,5 @@
 import functools
+import itertools
 import math
 
 import jax
@@ -49,6 +50,7 @@
 
 
 MESH = pl.DeviceIdType.MESH
+LANES = 128
 VMEM = pl.BlockSpec(memory_space=pltpu.VMEM)
 
 
@@ -268,6 +270,331 @@
             collective_id=number, has_side_effects=True, vmem_limit_bytes=40 * 1024 * 1024
         ),
     )(parts)
+
+
+def divide(width, choices=(256, 128)):
+    for part in choices:
+        if width % part == 0 and width // part >= 1:
+            return part
+    return width
+
+
+def moe_kernel(
+    groups,
+    ranks,
+    cores,
+    pieces,
+    depths,
+    tokens,
+    select,
+    resid,
+    weights,
+    gate_hbm,
+    up_hbm,
+    down_hbm,
+    mixed,
+    send,
+    recv,
+    near,
+    mid,
+    home,
+    rows,
+    gate_w,
+    up_w,
+    down_w,
+    found,
+    gate_acc,
+    up_acc,
+    slab,
+    sems,
+    load_sems,
+    own_sem,
+):
+    tok, mdl = lax.axis_index("tok"), lax.axis_index("mdl")
+    group, rank = tok // ranks, tok % ranks
+    toks = groups * ranks
+    main = send.shape[1]
+    cap = select.shape[0] // groups
+    rest = cap - main
+    width = tokens.shape[1]
+    hidden = slab.shape[1]
+    part = width // pieces
+    columns = cut(width, pieces)
+    packed = cut(send.shape[2], pieces)
+    blocks = rest * part // main // LANES * (main // rest)
+    main_rows = cores * toks * main
+
+    def pack(target, lead, rows_in, row, c):
+        for b in range(blocks):
+            spot, lane = divmod(b, main // rest)
+            at = c * (send.shape[2] // pieces) + part + spot * LANES
+            target[(*lead, pl.ds(lane * rest, rest), pl.ds(at, LANES))] = rows_in[
+                row : row + rest, b * LANES : (b + 1) * LANES
+            ]
+
+    def unpack(target, row, source, lead, c):
+        for b in range(blocks):
+            spot, lane = divmod(b, main // rest)
+            at = c * (send.shape[2] // pieces) + part + spot * LANES
+            target[row : row + rest, b * LANES : (b + 1) * LANES] = source[
+                (*lead, pl.ds(lane * rest, rest), pl.ds(at, LANES))
+            ]
+
+    def body(c):
+        return pl.ds(c * (send.shape[2] // pieces), part)
+
+    tile = divide(hidden)
+
+    loads = {}
+
+    def load(name, c, src, dst):
+        copy = pltpu.make_async_copy(src, dst, load_sems.at[len(loads)])
+        copy.start()
+        loads[name, c] = copy
+
+    for c in range(pieces):
+        load("gate", c, gate_hbm.at[0, columns[c], :], gate_w.at[columns[c], :])
+        load("up", c, up_hbm.at[0, columns[c], :], up_w.at[columns[c], :])
+    for c in range(pieces):
+        load("down", c, down_hbm.at[0, :, columns[c]], down_w.at[c])
+
+    greet(peers_of(groups, ranks, True))
+    started = []
+    numbers = itertools.count()
+
+    def go(src, dst, device):
+        copy = remote(src, dst, sems, next(numbers), device)
+        started.append(copy)
+        return copy
+
+    other = place(tok, 1 - mdl)
+
+    def rank_place(r):
+        return place(group * ranks + (rank + r) % ranks, mdl)
+
+    def group_place(g):
+        return place((group + g) % groups * ranks + rank, mdl)
+
+    far = near_first(groups)
+    near_ranks = near_first(ranks)
+    by_group, by_rank, by_core = {}, {}, {}
+    for c in range(pieces):
+        picked = jnp.dot(
+            select[...], tokens[:, columns[c]], preferred_element_type=jnp.float32
+        ).astype(send.dtype)
+        for e in range(groups):
+            send[e, :, body(c)] = picked[e * main : (e + 1) * main]
+            pack(send, (e,), picked, groups * main + e * rest, c)
+        for d in far:
+            by_group[c, d] = go(
+                send.at[(group + d) % groups, :, packed[c]],
+                recv.at[mdl, group, rank, :, packed[c]],
+                group_place(d),
+            )
+        for r in near_ranks:
+            by_rank[c, 0, r] = go(
+                send.at[group, :, packed[c]],
+                recv.at[mdl, group, rank, :, packed[c]],
+                rank_place(r),
+            )
+        by_core[c, 0, 0] = go(
+            send.at[group, :, packed[c]], recv.at[mdl, group, rank, :, packed[c]], other
+        )
+
+    own = pltpu.make_async_copy(send.at[group], recv.at[mdl, group, rank], own_sem)
+    own.start()
+
+    def from_groups(c):
+        for d in far:
+            by_group[c, d].wait_recv()
+            source = (group + groups - d) % groups
+            block = recv.at[mdl, source, rank, :, packed[c]]
+            for r in near_ranks:
+                by_rank[c, d, r] = go(block, block, rank_place(r))
+            by_core[c, d, 0] = go(block, block, other)
+
+    def from_ranks(c):
+        for d in [0] + far:
+            for r in near_ranks:
+                by_rank[c, d, r].wait_recv()
+                source = (group + groups - d) % groups
+                giver = (rank + ranks - r) % ranks
+                block = recv.at[mdl, source, giver, :, packed[c]]
+                by_core[c, d, r] = go(block, block, other)
+
+    def assemble(c):
+        for d in [0] + far:
+            for r in [0] + near_ranks:
+                by_core[c, d, r].wait_recv()
+        if c == 0:
+            own.wait()
+        rows[0:main_rows, :] = recv[:, :, :, :, body(c)].reshape(main_rows, part)
+        spot = main_rows
+        for m in range(cores):
+            for g in range(groups):
+                for r in range(ranks):
+                    unpack(rows, spot, recv, (m, g, r), c)
+                    spot += rest
+
+    def project(c):
+        assemble(c)
+        loads["gate", c].wait()
+        loads["up", c].wait()
+
+        def step(n, carry):
+            at = pl.ds(pl.multiple_of(n * tile, tile), tile)
+            x = rows[...]
+            gate_val = jnp.dot(x, gate_w[columns[c], at], preferred_element_type=jnp.float32)
+            up_val = jnp.dot(x, up_w[columns[c], at], preferred_element_type=jnp.float32)
+            if c > 0:
+                gate_val = gate_val + gate_acc[:, at]
+                up_val = up_val + up_acc[:, at]
+            if c < pieces - 1:
+                gate_acc[:, at] = gate_val
+                up_acc[:, at] = up_val
+            else:
+                slab[:, at] = (gate_val / (1.0 + jnp.exp(-gate_val)) * up_val).astype(slab.dtype)
+            return carry
+
+        lax.fori_loop(0, hidden // tile, step, 0)
+
+    for s in range(pieces + 2):
+        if s < pieces:
+            from_groups(s)
+        if 0 <= s - 1 < pieces:
+            from_ranks(s - 1)
+        if 0 <= s - 2 < pieces:
+            project(s - 2)
+
+    for copy in started:
+        copy.wait_send()
+    started.clear()
+    down_tile = divide(part)
+    across, to_rank, to_home = {}, {}, {}
+
+    def down(c):
+        loads["down", c].wait()
+
+        def step(n, carry):
+            at = pl.multiple_of(n * down_tile, down_tile)
+            rows[:, pl.ds(at, down_tile)] = jnp.dot(
+                slab[...],
+                down_w[c, :, pl.ds(at, down_tile)],
+                preferred_element_type=jnp.float32,
+            ).astype(rows.dtype)
+            return carry
+
+        lax.fori_loop(0, part // down_tile, step, 0)
+        recv[:, :, :, :, body(c)] = rows[0:main_rows, :].reshape(cores, groups, ranks, main, part)
+        spot = main_rows
+        for m in range(cores):
+            for g in range(groups):
+                for r in range(ranks):
+                    pack(recv, (m, g, r), rows, spot, c)
+                    spot += rest
+        across[c] = go(
+            recv.at[1 - mdl, :, :, :, packed[c]], near.at[:, :, :, packed[c]], other
+        )
+
+    def pair(g, r, c):
+        return recv[mdl, g, r, :, packed[c]].astype(jnp.float32) + near[
+            g, r, :, packed[c]
+        ].astype(jnp.float32)
+
+    def to_ranks(c):
+        across[c].wait_recv()
+        for r in near_ranks:
+            there = (rank + r) % ranks
+            for g in range(groups):
+                recv[mdl, g, there, :, packed[c]] = pair(g, there, c).astype(recv.dtype)
+            to_rank[c, r] = go(
+                recv.at[mdl, :, there, :, packed[c]], mid.at[r - 1, :, :, packed[c]], rank_place(r)
+            )
+
+    def to_sources(c):
+        for r in near_ranks:
+            to_rank[c, r].wait_recv()
+        for d in far[::-1] + [0]:
+            there = (group + d) % groups
+            total = pair(there, rank, c)
+            for r in near_ranks:
+                total = total + mid[r - 1, there, :, packed[c]].astype(jnp.float32)
+            if d == 0:
+                home[group, :, packed[c]] = total.astype(home.dtype)
+            else:
+                recv[mdl, there, rank, :, packed[c]] = total.astype(recv.dtype)
+                to_home[c, d] = go(
+                    recv.at[mdl, there, rank, :, packed[c]],
+                    home.at[group, :, packed[c]],
+                    group_place(d),
+                )
+
+    def finish(c):
+        for d in far:
+            to_home[c, d].wait_recv()
+        found[0 : groups * main, :] = home[:, :, body(c)].reshape(groups * main, part)
+        for e in range(groups):
+            unpack(found, groups * main + e * rest, home, (e,), c)
+        terms = jnp.dot(weights[...], found[...], preferred_element_type=jnp.float32)
+        total = resid[:, columns[c]]
+        for k in range(weights.shape[0] // resid.shape[0]):
+            total = total + terms[k * resid.shape[0] : (k + 1) * resid.shape[0]]
+        mixed[:, columns[c]] = total.astype(mixed.dtype)
+
+    lag_rank, lag_source, lag_end = depths
+    for s in range(pieces + lag_end):
+        if s < pieces:
+            down(s)
+        if 0 <= s - lag_rank < pieces:
+            to_ranks(s - lag_rank)
+        if 0 <= s - lag_source < pieces:
+            to_sources(s - lag_source)
+        if 0 <= s - lag_end < pieces:
+            finish(s - lag_end)
+    for copy in started:
+        copy.wait_send()
+
+
+def experts(
+    tokens, select, resid, weights, w_gate, w_up, w_down, groups, ranks, cores, number, pieces=4
+):
+    width = tokens.shape[1]
+    toks = groups * ranks
+    cap = select.shape[0] // groups
+    main = cap // 16 * 16
+    packed = width // main * cap
+    depth, hidden = w_gate.shape[1:]
+    part = width // pieces
+    dtype = tokens.dtype
+    copies = pieces * ((groups - 1) * 2 + (groups + 1) * (ranks - 1) + toks + 1)
+    total_rows = cores * toks * cap
+    return pl.pallas_call(
+        functools.partial(moe_kernel, groups, ranks, cores, pieces, (1, 2, 4)),
+        out_shape=jax.ShapeDtypeStruct(resid.shape, dtype),
+        in_specs=[VMEM] * 4 + [pl.BlockSpec(memory_space=pl.ANY)] * 3,
+        out_specs=VMEM,
+        scratch_shapes=[
+            pltpu.VMEM((groups, main, packed), dtype),
+            pltpu.VMEM((cores, groups, ranks, main, packed), dtype),
+            pltpu.VMEM((groups, ranks, main, packed), dtype),
+            pltpu.VMEM((max(ranks - 1, 1), groups, main, packed), dtype),
+            pltpu.VMEM((groups, main, packed), dtype),
+            pltpu.VMEM((total_rows, part), dtype),
+            pltpu.VMEM((depth, hidden), dtype),
+            pltpu.VMEM((depth, hidden), dtype),
+            pltpu.VMEM((pieces, hidden, part), dtype),
+            pltpu.VMEM((groups * cap, part), dtype),
+            pltpu.VMEM((total_rows, hidden), jnp.float32),
+            pltpu.VMEM((total_rows, hidden), jnp.float32),
+            pltpu.VMEM((total_rows, hidden), dtype),
+            pltpu.SemaphoreType.DMA((2, copies)),
+            pltpu.SemaphoreType.DMA((3 * pieces,)),
+            pltpu.SemaphoreType.DMA,
+        ],
+        compiler_params=pltpu.CompilerParams(
+            collective_id=number, has_side_effects=True, vmem_limit_bytes=67043328
+        ),
+    )(tokens, select, resid, weights, w_gate, w_up, w_down)
 
 
 def attention_kernel(length, queries, cached, fresh, out):
@@ -391,22 +718,35 @@
     capacity = core_rows * TOPK * 9 // (8 * EXPERTS)
     slot_range = jnp.arange(capacity)
     select = (slot_of.T[:, None, :] == slot_range[None, :, None]) & (chosen.T[:, None, :] > 0)
-    send_rows = jnp.einsum(
-        "eci,id->ecd", select.astype(jnp.bfloat16), moe_in, preferred_element_type=jnp.float32
-    ).astype(jnp.bfloat16)
-    model_width = moe_in.shape[1]
-    received = spread(send_rows, EXPERTS, ranks, True, False, 5, 4)
-    flat_rows = received.reshape(-1, model_width)
-    gate_val = jnp.dot(flat_rows, w_gate[0], preferred_element_type=jnp.float32)
-    up_val = jnp.dot(flat_rows, w_up[0], preferred_element_type=jnp.float32)
-    slab_hidden = (jax.nn.silu(gate_val) * up_val).astype(jnp.bfloat16)
-    slab_out = jnp.dot(slab_hidden, w_down[0], preferred_element_type=jnp.float32).astype(
-        jnp.bfloat16
-    )
-    summed = collect(slab_out.reshape(received.shape), EXPERTS, ranks, 6, 4).astype(jnp.float32)
-    weight_table = select.astype(jnp.float32) * route.T[:, None, :]
-    moe_out = jnp.einsum("eci,ecd->id", weight_table, summed, precision=lax.Precision.HIGHEST)
-    mixed = (resid + moe_out).astype(jnp.bfloat16)
+    main = capacity // 16 * 16
+
+    def by_tile(table):
+        return jnp.concatenate(
+            [
+                table[:, :main].reshape(EXPERTS * main, core_rows),
+                table[:, main:].reshape(EXPERTS * (capacity - main), core_rows),
+            ]
+        )
+
+    picks = by_tile(select.astype(jnp.float32))
+    table = by_tile(select.astype(jnp.float32) * route.T[:, None, :]).T
+    first = table.astype(jnp.bfloat16)
+    second = (table - first.astype(jnp.float32)).astype(jnp.bfloat16)
+    third = (table - first.astype(jnp.float32) - second.astype(jnp.float32)).astype(jnp.bfloat16)
+    weights = jnp.concatenate([first, second, third])
+    mixed = experts(
+        moe_in,
+        picks.astype(jnp.bfloat16),
+        resid,
+        weights,
+        w_gate,
+        w_up,
+        w_down,
+        EXPERTS,
+        ranks,
+        core_count,
+        5,
+    )
     return (mixed, fresh_key_value)
 
 

time: 157 us -> 138 us (0.88)
  matrix products: 26.6 us -> 1.14 us
  Pallas kernels: 114 us -> 119 us
  other arithmetic: 1.84 us -> 4.69 us
  local copies, waits for them, and re-layouts: 10.2 us -> 8.61 us
    pallas_call x0 -> x1, Pallas kernels: none -> 58.2 us  [experts(): pl.pallas_call(functools.partial(moe_kernel, groups, ranks, cores, pieces...]
    pallas_call x4 -> x3, Pallas kernels: 75.9 us -> 48 us  [spread(): pl.pallas_call(functools.partial(spread_kernel, groups, ranks, cores, sam...]
    pallas_call x2 -> x1, Pallas kernels: 36 us -> 10.4 us  [collect(): pl.pallas_call(functools.partial(collect_kernel, groups, ranks, pieces),...]
    dot_general x5 -> x0, matrix products: 25.4 us -> none  [the longest x1 9.85 us: shards(): up_val = jnp.dot(flat_rows, w_up[0], preferred_element_type=jnp.float32)]
    reshape x2, local copies, waits for them, and re-layouts: 4.71 us -> 0.14 us  [the longest x1 0.08 us: by_tile(): table[:, main:].reshape(EXPERTS * (capacity - main), core_rows)]
    unnamed x39 -> x16, local copies, waits for them, and re-layouts: 4.86 us -> 6.78 us
where the time goes in v1:
time: 138 us; the launch traced here: 137 us
  Pallas kernels  119 us (86%)
  local copies, waits for them, and re-layouts  8.61 us (6%)
  other arithmetic  4.69 us (3%)
  blocking collectives  2.64 us (2%)
  between operations  1.57 us (1%)
    pallas_call x1, Pallas kernels, experts(): pl.pallas_call(functools.partial(moe_kernel, groups, ranks, cores, pieces...  58.2 us
    pallas_call x3, Pallas kernels, spread(): pl.pallas_call(functools.partial(spread_kernel, groups, ranks, cores, sam...  48 us
    pallas_call x1, Pallas kernels, collect(): pl.pallas_call(functools.partial(collect_kernel, groups, ranks, pieces),...  10.4 us
    unnamed x16, local copies, waits for them, and re-layouts  6.78 us

profile of v1, /device:TPU:0, one launch (start us, length us, event | category | flops | bytes accessed | tf_op | source)
XLA Modules:
  0.0 137.5 jit_solution(2153021084655891589)
XLA Ops:
  0.7 2.6 %all_gather.3 = bf16[64,4096]{1,0:T(8,128)(2,1)S(1)} all-gather(bf16[64,2048]{1,0:T(8,128)(2,1)} %param.13), channel_id=1, replica_groups=mesh['grp'=2,'tok'=8,'mdl'=2] {'mdl'}, dimensions={1}, use_global_device_ids=true | all-gather | bytes 786432 | tf_op jit(solution)/shard_map/all_gather | solution.py:674
  3.3 0.2 fusion
  3.5 0.7 convert_element_type.67
  4.2 0.1 fusion.2
  4.4 14.0 %shard_map.140 = bf16[8,2,32,512]{3,2,1,0:T(8,128)(2,1)S(1)} custom-call(bf16[8,32,512]{2,1,0:T(8,128)(2,1)S(1)} %bitcast.57), custom_call_target="tpu_custom_call" | custom-call | tf_op jit(solution)/shard_map/pallas_call | solution.py:165
  18.4 1.2 reshape.128
  19.6 0.4 convolution_convert_fusion
  20.1 15.9 %shard_map.141 = bf16[8,64,512]{2,1,0:T(8,128)(2,1)S(1)} custom-call(bf16[8,64,512]{2,1,0:T(8,128)(2,1)S(1)} %bitcast.56), custom_call_target="tpu_custom_call" | custom-call | tf_op jit(solution)/shard_map/pallas_call | solution.py:165
  36.1 0.1 reshape.130
  36.9 0.2 multiply_cosine_fusion
  37.1 0.1 subtract_convert_fusion
  37.2 0.1 maximum_bitcast_fusion
  37.4 0.6 pad_maximum_fusion
  38.0 1.9 %copy.92 = bf16[1,2048,2,2,128]{4,1,3,2,0:T(8,128)(2,1)S(1)} copy(bf16[1,2048,2,2,128]{4,3,2,1,0:T(2,128)(2,1)} %param.15) | data formatting | bytes 4194304 | tf_op args[2]
  39.9 0.9 copy.94
  40.8 2.2 %shard_map.142.send = bf16[64,1024]{1,0:T(8,128)(2,1)S(1)} custom-call(s32[1]{0:T(128)} %copy.97.length, bf16[8,64,128]{2,1,0:T(8,128)(2,1)S(1)} %bitcast.60, bf16[2,2,2048,128]{3,2,1,0:T(8,128)(2,1)S(1)} %bitcast.54, bf16[2,2,64,128]{3,2,1,0:T(8,128)(2,1)S(1)} %get-tuple-element.17.fresh), custom_call_target="tpu_custom_call" | custom-call | tf_op jit(solution)/shard_map/pallas_call | solution.py:639
  43.0 18.1 %shard_map.143 = bf16[8,64,1024]{2,1,0:T(8,128)(2,1)S(1)} custom-call(bf16[64,1024]{1,0:T(8,128)(2,1)S(1)} %shard_map.142.send), custom_call_target="tpu_custom_call" | custom-call | tf_op jit(solution)/shard_map/pallas_call | solution.py:165
  61.1 0.7 convolution_convert_fusion.1
  61.8 10.4 %shard_map.144 = bf16[8,32,512]{2,1,0:T(8,128)(2,1)S(1)} custom-call(bf16[8,2,32,512]{3,2,1,0:T(8,128)(2,1)S(1)} %bitcast.59), custom_call_target="tpu_custom_call" | custom-call | tf_op jit(solution)/shard_map/pallas_call | solution.py:258
  72.3 0.2 multiply_reduce_fusion
  72.6 0.8 copy-done
  73.3 0.8 multiply_convert_fusion.tokens
  74.1 0.1 copy.76
  74.3 0.1 copy.78
  74.5 0.1 copy.80
  74.6 0.1 fusion.5
  74.7 0.1 fusion.6
  74.8 0.6 pad_maximum_fusion.1.weights
  75.4 0.6 pad_maximum_fusion.2.select
  76.0 58.2 %shard_map.145 = bf16[32,4096]{1,0:T(8,128)(2,1)} custom-call(bf16[32,4096]{1,0:T(8,128)(2,1)} %multiply_convert_fusion.tokens, bf16[72,32]{1,0:T(8,128)(2,1)} %pad_maximum_fusion.2.select, f32[32,4096]{1,0:T(8,128)} %copy-done, bf16[96,72]{1,0:T(8,128)(2,1)} %pad_maximum_fusion.1.weights, bf16[1,4096,1792]{2,1,0:T(8,128)(2,1)} %gate_hbm.1, ...), custom_call_target="tpu_custom_call" | custom-call | tf_op jit(solution)/shard_map/pallas_call | solution.py:571
  134.3 1.5 %copy.81 = bf16[64,2,2,128]{3,2,1,0:T(2,128)(2,1)} copy(bf16[64,2,2,128]{3,0,2,1:T(8,128)(2,1)} %get-tuple-element.16) | data formatting | bytes 131072
  135.8 1.7 %copy.98 = bf16[32,4096]{1,0:T(8,128)(2,1)} copy(bf16[32,4096]{1,0:T(8,128)(2,1)} %shard_map.145) | data formatting | bytes 524288
  (34 shorter events, 0.6 us)
Async XLA Ops:
  0.6 60.5 %copy-start.4 = (bf16[8,128,512]{2,1,0:T(8,128)(2,1)S(1)}, bf16[8,128,512]{2,1,0:T(8,128)(2,1)}, u32[]{:S(2)}) copy-start(bf16[8,128,512]{2,1,0:T(8,128)(2,1)} %param.18) | copy-start | bytes 3145732
  0.6 71.9 %copy-start.1 = (bf16[4096]{0:T(1024)(128)(2,1)S(1)}, bf16[4096]{0:T(1024)(128)(2,1)}, u32[]{:S(2)}) copy-start(bf16[4096]{0:T(1024)(128)(2,1)} %param.20) | copy-start | bytes 24580
  0.7 73.5 %copy-start.2 = (s32[32,2]{0,1:T(2,128)S(1)}, s32[32,2]{0,1:T(2,128)}, u32[]{:S(2)}) copy-start(s32[32,2]{0,1:T(2,128)} %param.24) | copy-start | bytes 772
  0.7 73.7 %copy-start.3 = (f32[32,2]{0,1:T(2,128)S(1)}, f32[32,2]{0,1:T(2,128)}, u32[]{:S(2)}) copy-start(f32[32,2]{0,1:T(2,128)} %param.25) | copy-start | bytes 772
  72.5 0.8 copy-start

commit v2 on v1

v2 whole, which is shorter than its diff:
```python
import functools
import itertools
import math

import jax
import jax.numpy as jnp
from jax import lax
from jax.experimental import pallas as pl
from jax.experimental.pallas import tpu as pltpu
from jax.sharding import PartitionSpec as P

EXPERTS = 4
TOPK = 2
PIECES = 4


eps_norm = 1e-05
rope_base = 1000000.0
mask_fill = -1e30


def rotation(head_dim, positions):
    half_dim = head_dim // 2
    inverse = jnp.exp(
        jnp.arange(half_dim, dtype=jnp.float32) * (-2.0 * math.log(rope_base) / head_dim)
    )
    angle = positions.astype(jnp.float32)[:, None] * inverse[None, :]
    cosine, sine = jnp.cos(angle), jnp.sin(angle)
    return jnp.concatenate([cosine, cosine], axis=1), jnp.concatenate([-sine, sine], axis=1)


def score_rows(query_rows, key_rows, scale_factor):
    return (
        lax.dot_general(
            query_rows, key_rows, (((1,), (1,)), ((), ())), preferred_element_type=jnp.float32
        )
        * scale_factor
    )


MESH = pl.DeviceIdType.MESH
LANES = 128
VMEM = pl.BlockSpec(memory_space=pltpu.VMEM)


def place(tok, mdl):
    return (lax.axis_index("grp"), tok, mdl)


def greet(peers):
    barrier = pltpu.get_barrier_semaphore()
    for peer in peers:
        pl.semaphore_signal(barrier, inc=1, device_id=peer, device_id_type=MESH)
    pl.semaphore_wait(barrier, len(peers))


def peers_of(groups, ranks, cores):
    tok, mdl = lax.axis_index("tok"), lax.axis_index("mdl")
    group, rank = tok // ranks, tok % ranks
    peers = [place((group + d) % groups * ranks + rank, mdl) for d in range(1, groups)]
    peers += [place(group * ranks + (rank + d) % ranks, mdl) for d in range(1, ranks)]
    if cores:
        peers.append(place(tok, 1 - mdl))
    return peers


def remote(src, dst, sems, index, device):
    copy = pltpu.make_async_remote_copy(
        src_ref=src,
        dst_ref=dst,
        send_sem=sems.at[0, index],
        recv_sem=sems.at[1, index],
        device_id=device,
        device_id_type=MESH,
    )
    copy.start()
    return copy


def near_first(count):
    return sorted(range(1, count), key=lambda d: (min(d, count - d), d))


def cut(width, pieces):
    part = width // pieces
    return [pl.ds(c * part, part) for c in range(pieces)]


def divide(width, choices=(256, 128)):
    for part in choices:
        if width % part == 0 and width // part >= 1:
            return part
    return width


def layer_kernel(
    dims,
    lengths,
    hidden,
    queries,
    cosines,
    sines,
    attn_gain,
    moe_gain,
    select,
    weights,
    cache_hbm,
    wkv_hbm,
    wo_hbm,
    gate_hbm,
    up_hbm,
    down_hbm,
    mixed,
    fresh,
    full,
    slices,
    own_square,
    other_square,
    part_kv,
    mid_kv,
    sum_kv,
    in_kv,
    cache,
    wkv,
    wo,
    tops,
    sums,
    heads_acc,
    heads,
    part_out,
    near_out,
    in_out,
    resid,
    send,
    recv,
    near,
    mid,
    home,
    rows,
    gate_w,
    up_w,
    down_w,
    gate_acc,
    up_acc,
    slab,
    sems,
    load_sems,
):
    groups, ranks, cores, pieces = dims
    tok, mdl = lax.axis_index("tok"), lax.axis_index("mdl")
    group, rank = tok // ranks, tok % ranks
    toks = groups * ranks
    f32, narrow = jnp.float32, jnp.bfloat16

    width = full.shape[1]
    part = width // pieces
    columns = cut(width, pieces)
    loads = {}

    def load(src, dst, *name):
        copy = pltpu.make_async_copy(src, dst, load_sems.at[len(loads)])
        copy.start()
        loads[name] = copy

    load(wkv_hbm, wkv, "wkv")
    for h in range(cache.shape[0]):
        load(cache_hbm.at[h], cache.at[h], "cache", h)
    load(wo_hbm, wo, "wo")

    numbers = itertools.count()
    started = []
    other = place(tok, 1 - mdl)
    far = near_first(groups)
    near_ranks = near_first(ranks)
    every_rank = [0] + near_ranks

    def go(src, dst, device):
        copy = remote(src, dst, sems, next(numbers), device)
        started.append(copy)
        return copy

    def all_sent():
        for copy in started:
            copy.wait_send()
        started.clear()

    def rank_place(r):
        return place(group * ranks + (rank + r) % ranks, mdl)

    def group_place(g):
        return place((group + g) % groups * ranks + rank, mdl)

    def group_from(d):
        return (group + groups - d) % groups

    def rank_from(r):
        return (rank + ranks - r) % ranks

    greet(peers_of(toks, 1, True))

    span, features = hidden.shape
    half = span // cores
    depth = width // toks

    def lines(core):
        return pl.ds(pl.multiple_of(core * half, half), half)

    def half_features(core):
        return pl.ds(pl.multiple_of(core * features, features), features)

    swap = go(hidden.at[lines(1 - mdl), :], full.at[:, half_features(mdl)], other)
    full[:, half_features(mdl)] = hidden[lines(mdl), :]
    values = hidden[...].astype(f32)
    square = jnp.sum(values * values, axis=1, keepdims=True)
    own_square[...] = jnp.broadcast_to(square, own_square.shape)
    swap_square = go(own_square, other_square, other)
    for c in range(pieces):
        load(gate_hbm.at[0, columns[c], :], gate_w.at[columns[c], :], "gate", c)
        load(up_hbm.at[0, columns[c], :], up_w.at[columns[c], :], "up", c)
    for c in range(pieces):
        load(down_hbm.at[0, :, columns[c]], down_w.at[c], "down", c)
    swap.wait_recv()

    def slice_of(target):
        return pl.ds(pl.multiple_of(target * depth, depth), depth)

    outward, twin = {}, {}
    for d in [0] + far:
        for r in every_rank:
            target = (group + d) % groups * ranks + (rank + r) % ranks
            if d or r:
                outward[d, r] = go(
                    full.at[:, slice_of(target)],
                    slices.at[group, rank, mdl],
                    place(target, mdl),
                )
    slices[group, rank, mdl] = full[:, slice_of(tok)]
    twin[0, 0] = go(full.at[:, slice_of(tok)], slices.at[group, rank, mdl], other)

    query_heads, _, head_dim = queries.shape
    kv_heads = cache.shape[0]
    per_head = query_heads // kv_heads
    scale_factor = 1.0 / math.sqrt(head_dim)
    limit = cache.shape[2]
    block = min(512, limit)
    query_count = per_head * span

    def query_rows(h):
        return queries[h * per_head : (h + 1) * per_head].reshape(query_count, head_dim)

    def cached_attention(h):
        loads["cache", h].wait()
        asked = query_rows(h)
        scores, values = [], []
        for start in range(0, limit, block):
            position = lax.broadcasted_iota(jnp.int32, (query_count, block), 1) + start
            score = score_rows(asked, cache[h, 0, pl.ds(start, block)], scale_factor)
            scores.append(jnp.where(position < lengths[0], score, mask_fill))
            values.append(cache[h, 1, pl.ds(start, block)])
        top = functools.reduce(jnp.maximum, [jnp.max(x, axis=1, keepdims=True) for x in scores])
        total = jnp.zeros((query_count, 1), f32)
        found_values = jnp.zeros((query_count, head_dim), f32)
        for score, value_rows in zip(scores, values):
            chance = jnp.exp(score - top)
            total += jnp.sum(chance, axis=1, keepdims=True)
            found_values += jnp.dot(chance.astype(narrow), value_rows, preferred_element_type=f32)
        tops[h] = jnp.broadcast_to(top, (query_count, head_dim))
        sums[h] = jnp.broadcast_to(total, (query_count, head_dim))
        heads_acc[h] = found_values

    cached_attention(0)

    kv_width = wkv.shape[1]
    gain_slice = attn_gain[:, slice_of(tok)].astype(f32)
    loads["wkv",].wait()
    kv_rank, kv_home = {}, {}

    def project_kv(d):
        source = group_from(d)
        for r in every_rank:
            if d or r:
                outward[d, r].wait_recv()
                landed = slices.at[source, rank_from(r), mdl]
                twin[d, r] = go(landed, landed, other)
        for r in every_rank:
            twin[d, r].wait_recv()
        taken = slices[source].reshape(ranks * span, depth).astype(f32) * gain_slice
        part_kv[source] = (
            jnp.dot(taken.astype(narrow), wkv[...], preferred_element_type=f32)
            .astype(narrow)
            .reshape(ranks, span, kv_width)
        )
        for r in near_ranks:
            kv_rank[d, r] = go(
                part_kv.at[source, (rank + r) % ranks], mid_kv.at[r - 1, source], rank_place(r)
            )

    def reduce_kv(d):
        source = group_from(d)
        total = part_kv[source, rank].astype(f32)
        for r in near_ranks:
            kv_rank[d, r].wait_recv()
            total = total + mid_kv[r - 1, source].astype(f32)
        if d:
            sum_kv[source] = total.astype(narrow)
            kv_home[d] = go(sum_kv.at[source], in_kv.at[group], group_place(-d))
        else:
            in_kv[group] = total.astype(narrow)

    order = [0] + far
    for s in range(groups + 1):
        if s < groups:
            project_kv(order[s])
        if s > 0:
            reduce_kv(order[s - 1])
    for h in range(1, kv_heads):
        cached_attention(h)
    swap_square.wait_recv()
    meansq = (own_square[...] + other_square[...]) * (1.0 / width)
    row_scale = lax.rsqrt(meansq + eps_norm)
    for d in far:
        kv_home[d].wait_recv()

    token = lax.broadcasted_iota(jnp.int32, (query_count, span), 0) % span
    column = lax.broadcasted_iota(jnp.int32, (query_count, span), 1)
    head_width = per_head * head_dim
    head_columns = [pl.ds(h * head_width, head_width) for h in range(kv_heads)]
    head_group, head_rank = {}, {}
    for h in range(kv_heads):
        pair_of = []
        for kind in range(2):
            at = pl.ds((2 * h + kind) * head_dim, head_dim)
            total = in_kv[0, :, at].astype(f32)
            for g in range(1, groups):
                total = total + in_kv[g, :, at].astype(f32)
            total = total * row_scale
            if kind == 0:
                total = total * cosines[...] + pltpu.roll(total, head_dim // 2, 1) * sines[...]
            pair_of.append(total.astype(narrow))
            fresh[:, at] = pair_of[kind]
        score = score_rows(query_rows(h), pair_of[0], scale_factor)
        score = jnp.where(column <= token, score, mask_fill)
        before = tops[h]
        top = jnp.maximum(before, jnp.max(score, axis=1, keepdims=True))
        fade = jnp.exp(before - top)
        chance = jnp.exp(score - top[:, :1])
        total = sums[h] * fade + jnp.sum(chance, axis=1, keepdims=True)
        attended = heads_acc[h] * fade + jnp.dot(
            chance.astype(narrow), pair_of[1], preferred_element_type=f32
        )
        attended = (attended / total).astype(narrow)
        for head in range(per_head):
            at = pl.ds(h * head_width + head * head_dim, head_dim)
            heads[group, rank, :, at] = attended[head * span : (head + 1) * span]
        own = heads.at[group, rank, :, head_columns[h]]
        for d in far:
            head_group[h, d] = go(own, own, group_place(d))
        for r in near_ranks:
            head_rank[h, 0, r] = go(own, own, rank_place(r))

    out_width = wo.shape[1]
    loads["wo",].wait()
    out_core, out_home = {}, {}

    def forward_heads(d):
        for h in range(kv_heads):
            head_group[h, d].wait_recv()
            landed = heads.at[group_from(d), rank, :, head_columns[h]]
            for r in near_ranks:
                head_rank[h, d, r] = go(landed, landed, rank_place(r))

    def project_out(d):
        source = group_from(d)
        for h in range(kv_heads):
            for r in near_ranks:
                head_rank[h, d, r].wait_recv()
        part_out[source] = (
            jnp.dot(
                heads[source].reshape(ranks * span, heads.shape[3]),
                wo[...],
                preferred_element_type=f32,
            )
            .astype(narrow)
            .reshape(ranks, cores, half, out_width)
        )
        out_core[d] = go(part_out.at[source, :, 1 - mdl], near_out.at[source], other)

    def send_out(d):
        source = group_from(d)
        out_core[d].wait_recv()
        for r in every_rank:
            giver = rank_from(r)
            total = part_out[source, giver, mdl].astype(f32) + near_out[source, giver].astype(f32)
            if d or r:
                part_out[source, giver, mdl] = total.astype(narrow)
                out_home[d, r] = go(
                    part_out.at[source, giver, mdl],
                    in_out.at[tok],
                    place(source * ranks + giver, mdl),
                )
            else:
                in_out[tok] = total.astype(narrow)

    for s in range(groups + 2):
        if 0 < s < groups:
            forward_heads(order[s])
        if 0 <= s - 1 < groups:
            project_out(order[s - 1])
        if 0 <= s - 2 < groups:
            send_out(order[s - 2])
    for d in order:
        for r in every_rank:
            if d or r:
                out_home[d, r].wait_recv()
    square = jnp.zeros((half, 1), f32)
    for t in range(toks):
        at = pl.ds(t * depth, depth)
        total = full[:, at].astype(f32) + in_out[t].astype(f32)
        resid[:, at] = total
        square += jnp.sum(total * total, axis=1, keepdims=True)
    row_scale = lax.rsqrt(square * (1.0 / width) + eps_norm)
    all_sent()
    tokens = full
    tokens[...] = (resid[...] * row_scale * moe_gain[...].astype(f32)).astype(narrow)

    main = send.shape[1]
    cap = select.shape[0] // groups
    rest = cap - main
    hidden_units = slab.shape[1]
    packed = cut(send.shape[2], pieces)
    blocks = part // LANES
    main_rows = cores * toks * main
    tile = divide(hidden_units)

    def pack(target, lead, rows_in, row, c):
        for b in range(blocks):
            spot, lane = divmod(b, main // rest)
            at = c * (send.shape[2] // pieces) + part + spot * LANES
            target[(*lead, pl.ds(lane * rest, rest), pl.ds(at, LANES))] = rows_in[
                row : row + rest, b * LANES : (b + 1) * LANES
            ]

    def unpack(target, row, source, lead, c):
        for b in range(blocks):
            spot, lane = divmod(b, main // rest)
            at = c * (send.shape[2] // pieces) + part + spot * LANES
            target[row : row + rest, b * LANES : (b + 1) * LANES] = source[
                (*lead, pl.ds(lane * rest, rest), pl.ds(at, LANES))
            ]

    def body(c):
        return pl.ds(c * (send.shape[2] // pieces), part)

    by_group, by_rank, by_core = {}, {}, {}
    for c in range(pieces):
        picked = jnp.dot(
            select[...], tokens[:, columns[c]], preferred_element_type=jnp.float32
        ).astype(send.dtype)
        for e in range(groups):
            send[e, :, body(c)] = picked[e * main : (e + 1) * main]
            pack(send, (e,), picked, groups * main + e * rest, c)
        for d in far:
            by_group[c, d] = go(
                send.at[(group + d) % groups, :, packed[c]],
                recv.at[mdl, group, rank, :, packed[c]],
                group_place(d),
            )
        for r in near_ranks:
            by_rank[c, 0, r] = go(
                send.at[group, :, packed[c]],
                recv.at[mdl, group, rank, :, packed[c]],
                rank_place(r),
            )
        by_core[c, 0, 0] = go(
            send.at[group, :, packed[c]], recv.at[mdl, group, rank, :, packed[c]], other
        )

    recv[mdl, group, rank] = send[group]

    def from_groups(c):
        for d in far:
            by_group[c, d].wait_recv()
            source = (group + groups - d) % groups
            block = recv.at[mdl, source, rank, :, packed[c]]
            for r in near_ranks:
                by_rank[c, d, r] = go(block, block, rank_place(r))
            by_core[c, d, 0] = go(block, block, other)

    def from_ranks(c):
        for d in [0] + far:
            for r in near_ranks:
                by_rank[c, d, r].wait_recv()
                source = (group + groups - d) % groups
                giver = (rank + ranks - r) % ranks
                block = recv.at[mdl, source, giver, :, packed[c]]
                by_core[c, d, r] = go(block, block, other)

    def assemble(c):
        for d in [0] + far:
            for r in [0] + near_ranks:
                by_core[c, d, r].wait_recv()
        rows[0:main_rows, :] = recv[:, :, :, :, body(c)].reshape(main_rows, part)
        spot = main_rows
        for m in range(cores):
            for g in range(groups):
                for r in range(ranks):
                    unpack(rows, spot, recv, (m, g, r), c)
                    spot += rest

    def project(c):
        assemble(c)
        loads["gate", c].wait()
        loads["up", c].wait()

        def step(n, carry):
            at = pl.ds(pl.multiple_of(n * tile, tile), tile)
            x = rows[...]
            gate_val = jnp.dot(x, gate_w[columns[c], at], preferred_element_type=jnp.float32)
            up_val = jnp.dot(x, up_w[columns[c], at], preferred_element_type=jnp.float32)
            if c > 0:
                gate_val = gate_val + gate_acc[:, at]
                up_val = up_val + up_acc[:, at]
            if c < pieces - 1:
                gate_acc[:, at] = gate_val
                up_acc[:, at] = up_val
            else:
                slab[:, at] = (gate_val / (1.0 + jnp.exp(-gate_val)) * up_val).astype(slab.dtype)
            return carry

        lax.fori_loop(0, hidden_units // tile, step, 0)

    for s in range(pieces + 2):
        if s < pieces:
            from_groups(s)
        if 0 <= s - 1 < pieces:
            from_ranks(s - 1)
        if 0 <= s - 2 < pieces:
            project(s - 2)

    all_sent()
    down_tile = divide(part)
    across, to_rank, to_home = {}, {}, {}

    def down(c):
        loads["down", c].wait()

        def step(n, carry):
            at = pl.multiple_of(n * down_tile, down_tile)
            rows[:, pl.ds(at, down_tile)] = jnp.dot(
                slab[...],
                down_w[c, :, pl.ds(at, down_tile)],
                preferred_element_type=jnp.float32,
            ).astype(rows.dtype)
            return carry

        lax.fori_loop(0, part // down_tile, step, 0)
        recv[:, :, :, :, body(c)] = rows[0:main_rows, :].reshape(cores, groups, ranks, main, part)
        spot = main_rows
        for m in range(cores):
            for g in range(groups):
                for r in range(ranks):
                    pack(recv, (m, g, r), rows, spot, c)
                    spot += rest
        across[c] = go(
            recv.at[1 - mdl, :, :, :, packed[c]], near.at[:, :, :, packed[c]], other
        )

    def pair(g, r, c):
        return recv[mdl, g, r, :, packed[c]].astype(jnp.float32) + near[
            g, r, :, packed[c]
        ].astype(jnp.float32)

    def to_ranks(c):
        across[c].wait_recv()
        for r in near_ranks:
            there = (rank + r) % ranks
            for g in range(groups):
                recv[mdl, g, there, :, packed[c]] = pair(g, there, c).astype(recv.dtype)
            to_rank[c, r] = go(
                recv.at[mdl, :, there, :, packed[c]], mid.at[r - 1, :, :, packed[c]], rank_place(r)
            )

    def to_sources(c):
        for r in near_ranks:
            to_rank[c, r].wait_recv()
        for d in far[::-1] + [0]:
            there = (group + d) % groups
            total = pair(there, rank, c)
            for r in near_ranks:
                total = total + mid[r - 1, there, :, packed[c]].astype(jnp.float32)
            if d == 0:
                home[group, :, packed[c]] = total.astype(home.dtype)
            else:
                recv[mdl, there, rank, :, packed[c]] = total.astype(recv.dtype)
                to_home[c, d] = go(
                    recv.at[mdl, there, rank, :, packed[c]],
                    home.at[group, :, packed[c]],
                    group_place(d),
                )

    def finish(c):
        for d in far:
            to_home[c, d].wait_recv()
        rows[0 : groups * main, :] = home[:, :, body(c)].reshape(groups * main, part)
        for e in range(groups):
            unpack(rows, groups * main + e * rest, home, (e,), c)
        terms = jnp.dot(
            weights[...], rows[0 : groups * cap, :], preferred_element_type=jnp.float32
        )
        total = resid[:, columns[c]]
        for k in range(weights.shape[0] // resid.shape[0]):
            total = total + terms[k * resid.shape[0] : (k + 1) * resid.shape[0]]
        mixed[:, columns[c]] = total.astype(mixed.dtype)

    lag_rank, lag_source, lag_end = 1, 2, 4
    for s in range(pieces + lag_end):
        if s < pieces:
            down(s)
        if 0 <= s - lag_rank < pieces:
            to_ranks(s - lag_rank)
        if 0 <= s - lag_source < pieces:
            to_sources(s - lag_source)
        if 0 <= s - lag_end < pieces:
            finish(s - lag_end)
    all_sent()


def layer(
    dims,
    lengths,
    hidden,
    queries,
    cosines,
    sines,
    attn_gain,
    moe_gain,
    select,
    weights,
    cache,
    wkv,
    wo,
    w_gate,
    w_up,
    w_down,
):
    groups, ranks, cores, pieces = dims
    toks = groups * ranks
    span, features = hidden.shape
    half, width = span // cores, features * cores
    cap = select.shape[0] // groups
    main = cap // 16 * 16
    packed = width // main * cap
    depth, units = w_gate.shape[1:]
    part = width // pieces
    query_heads, _, head_dim = queries.shape
    kv_heads = cache.shape[0]
    query_count = query_heads // kv_heads * span
    kv_width, out_width = wkv.shape[1], wo.shape[1]
    dtype, f32 = hidden.dtype, jnp.float32
    total_rows = cores * toks * cap
    more = max(ranks - 1, 1)
    copies = (
        2
        + (2 * toks - 1)
        + groups * (ranks - 1)
        + groups
        - 1
        + kv_heads * (groups - 1 + groups * (ranks - 1))
        + groups
        + toks
        - 1
        + pieces * ((groups - 1) * 2 + (groups + 1) * (ranks - 1) + toks + 1)
    )
    remote_space = pl.BlockSpec(memory_space=pl.ANY)
    buffers = [
        ((half, width), dtype),
        ((groups, ranks, cores, half, wkv.shape[0]), dtype),
        ((span, head_dim), f32),
        ((span, head_dim), f32),
        ((groups, ranks, span, kv_width), dtype),
        ((more, groups, span, kv_width), dtype),
        ((groups, span, kv_width), dtype),
        ((groups, span, kv_width), dtype),
        (cache.shape, dtype),
        (wkv.shape, dtype),
        (wo.shape, dtype),
        ((kv_heads, query_count, head_dim), f32),
        ((kv_heads, query_count, head_dim), f32),
        ((kv_heads, query_count, head_dim), f32),
        ((groups, ranks, span, wo.shape[0]), dtype),
        ((groups, ranks, cores, half, out_width), dtype),
        ((groups, ranks, half, out_width), dtype),
        ((toks, half, out_width), dtype),
        ((half, width), f32),
        ((groups, main, packed), dtype),
        ((cores, groups, ranks, main, packed), dtype),
        ((groups, ranks, main, packed), dtype),
        ((more, groups, main, packed), dtype),
        ((groups, main, packed), dtype),
        ((total_rows, part), dtype),
        ((depth, units), dtype),
        ((depth, units), dtype),
        ((pieces, units, part), dtype),
        ((total_rows, units), f32),
        ((total_rows, units), f32),
        ((total_rows, units), dtype),
    ]
    return pl.pallas_call(
        functools.partial(layer_kernel, dims),
        out_shape=(
            jax.ShapeDtypeStruct((half, width), dtype),
            jax.ShapeDtypeStruct((span, kv_width), dtype),
        ),
        in_specs=[pl.BlockSpec(memory_space=pltpu.SMEM)] + [VMEM] * 8 + [remote_space] * 6,
        out_specs=(VMEM, VMEM),
        scratch_shapes=[pltpu.VMEM(shape, kind) for shape, kind in buffers]
        + [
            pltpu.SemaphoreType.DMA((2, copies)),
            pltpu.SemaphoreType.DMA((3 * pieces + kv_heads + 2,)),
        ],
        compiler_params=pltpu.CompilerParams(
            collective_id=1, has_side_effects=True, vmem_limit_bytes=67043328
        ),
    )(
        lengths,
        hidden,
        queries,
        cosines,
        sines,
        attn_gain,
        moe_gain,
        select,
        weights,
        cache,
        wkv,
        wo,
        w_gate,
        w_up,
        w_down,
    )


def shards(
    hidden,
    queries,
    cache,
    cache_lengths,
    wkv,
    wo,
    attn_gain,
    moe_gain,
    w_gate,
    w_up,
    w_down,
    expert_ids,
    gates,
):
    span_len = hidden.shape[0]
    toks = lax.axis_size("tok")
    core_count = lax.axis_size("mdl")
    ranks = toks // EXPERTS
    core_rows = span_len // core_count
    kv_heads, _, head_dim = wkv.shape[1:]
    positions = cache_lengths[0] + jnp.arange(span_len, dtype=jnp.int32)
    cosines, sines = rotation(head_dim, positions)
    expert_range = jnp.arange(EXPERTS)
    matches = expert_ids[:, :, None] == expert_range[None, None, :]
    chosen = jnp.sum(matches.astype(jnp.int32), axis=1)
    route = jnp.sum(jnp.where(matches, gates[:, :, None], 0.0), axis=1)
    slot_of = jnp.cumsum(chosen, axis=0) - chosen
    capacity = core_rows * TOPK * 9 // (8 * EXPERTS)
    slot_range = jnp.arange(capacity)
    select = (slot_of.T[:, None, :] == slot_range[None, :, None]) & (chosen.T[:, None, :] > 0)
    main = capacity // 16 * 16

    def by_tile(table):
        return jnp.concatenate(
            [
                table[:, :main].reshape(EXPERTS * main, core_rows),
                table[:, main:].reshape(EXPERTS * (capacity - main), core_rows),
            ]
        )

    picks = by_tile(select.astype(jnp.float32))
    table = by_tile(select.astype(jnp.float32) * route.T[:, None, :]).T
    first = table.astype(jnp.bfloat16)
    second = (table - first.astype(jnp.float32)).astype(jnp.bfloat16)
    third = (table - first.astype(jnp.float32) - second.astype(jnp.float32)).astype(jnp.bfloat16)
    weights = jnp.concatenate([first, second, third])
    mixed, fresh = layer(
        (EXPERTS, ranks, core_count, PIECES),
        cache_lengths,
        hidden,
        queries.transpose(1, 0, 2),
        cosines,
        sines,
        attn_gain[None],
        moe_gain[None],
        picks.astype(jnp.bfloat16),
        weights,
        cache[0].transpose(1, 2, 0, 3),
        wkv.reshape(wkv.shape[0], -1),
        wo.reshape(-1, wo.shape[2]),
        w_gate,
        w_up,
        w_down,
    )
    fresh_key_value = fresh.reshape(span_len, kv_heads, 2, head_dim)
    return (mixed, fresh_key_value)


def solution(mesh):
    in_specs = (
        P(("grp", "tok"), "mdl"),
        P(("grp", "tok"), "mdl", None),
        P(("grp", "tok"), None, "mdl", None, None),
        P(("grp", "tok")),
        P("tok", "mdl", None, None),
        P("mdl", None, "tok"),
        P(),
        P(),
        P(("tok", "mdl"), None, None),
        P(("tok", "mdl"), None, None),
        P(("tok", "mdl"), None, None),
        P(("grp", "tok", "mdl"), None),
        P(("grp", "tok", "mdl"), None),
    )
    out_specs = (P(("grp", "tok", "mdl"), None), P(("grp", "tok"), "mdl", None, None))
    return jax.shard_map(shards, mesh=mesh, in_specs=in_specs, out_specs=out_specs, check_vma=False)
```

time: 138 us -> 123 us (0.89)
  Pallas kernels: 119 us -> 105 us
  local copies, waits for them, and re-layouts: 8.61 us -> 12.9 us
  blocking collectives: 2.64 us -> 0 us
    pallas_call x6 -> x1, Pallas kernels: 119 us -> 105 us  [layer(): pl.pallas_call(functools.partial(layer_kernel, dims), out_shape=(jax.Shap...]
    all_gather x1 -> x0, blocking collectives: 2.64 us -> none  [shards(): full_rows = lax.all_gather(hidden, 'mdl', axis=1, tiled=True)]
    broadcast_in_dim x0 -> x2, local copies, waits for them, and re-layouts: none -> 2.63 us  [the longest x1 1.32 us: shards(): moe_gain[None]]
    reshape x3 -> x2, local copies, waits for them, and re-layouts: 1.35 us -> 3.52 us  [the longest x1 2.04 us: shards(): wkv.reshape(wkv.shape[0], -1)]
    convert_element_type x5 -> x1, other arithmetic: 1.66 us -> 0.01 us  [rotation(): angle = positions.astype(jnp.float32)[:, None] * inverse[None, :]]
    unnamed x16 -> x3, local copies, waits for them, and re-layouts: 6.78 us -> 6.46 us
where the time goes in v2:
time: 123 us
  Pallas kernels  105 us (85%)
  local copies, waits for them, and re-layouts  12.9 us (10%)
  other arithmetic  3.8 us (3%)
  between operations  1.35 us (1%)
    pallas_call x1, Pallas kernels, layer(): pl.pallas_call(functools.partial(layer_kernel, dims), out_shape=(jax.Shap...  105 us
    unnamed x3, local copies, waits for them, and re-layouts  6.46 us

profile of v2, /device:TPU:0, one launch (start us, length us, event | category | flops | bytes accessed | tf_op | source)
XLA Modules:
  0.0 123.0 jit_solution(13714285534018567409)
XLA Ops:
  1.3 0.7 convert_reduce_fusion
  2.0 0.7 select_reduce_fusion
  2.7 0.1 copy.52
  2.8 0.1 reduce_window_sum.11
  2.9 0.1 copy.54
  2.9 1.3 %broadcast_in_dim.16.attn_gain = bf16[1,4096]{1,0:T(2,128)(2,1)} reshape(bf16[4096]{0:T(1024)(128)(2,1)} %param.19) | data formatting | bytes 16384 | tf_op jit(solution)/shard_map/broadcast_in_dim | solution.py:797
  4.3 1.3 %broadcast_in_dim.17.moe_gain = bf16[1,4096]{1,0:T(2,128)(2,1)} reshape(bf16[4096]{0:T(1024)(128)(2,1)} %param.20) | data formatting | bytes 16384 | tf_op jit(solution)/shard_map/broadcast_in_dim | solution.py:798
  5.6 0.6 pad_maximum_fusion.3.select
  6.3 0.1 copy.55
  6.3 0.1 copy.56
  6.4 0.1 fusion.4
  6.5 0.1 fusion.2
  6.6 0.6 pad_maximum_fusion.2.weights
  7.2 0.2 fusion.3
  7.4 0.7 pad_maximum_fusion
  8.1 1.6 %copy.61 = bf16[64,8,128]{2,0,1:T(8,128)(2,1)} copy(bf16[64,8,128]{2,1,0:T(8,128)(2,1)} %param.14) | data formatting | bytes 262144 | tf_op args[1]
  9.7 2.0 %reshape.47.wkv_hbm = bf16[512,512]{1,0:T(8,128)(2,1)} reshape(bf16[512,2,2,128]{3,2,1,0:T(2,128)(2,1)} %param.17) | data formatting | bytes 1048576 | tf_op jit(solution)/shard_map/reshape | solution.py:802
  11.7 3.2 %copy.60 = bf16[1,2048,2,2,128]{4,1,3,2,0:T(8,128)(2,1)} copy(bf16[1,2048,2,2,128]{4,3,2,1,0:T(2,128)(2,1)} %param.15) | data formatting | bytes 4194304 | tf_op args[2]
  14.9 104.9 %shard_map.140 = (bf16[32,4096]{1,0:T(8,128)(2,1)}, bf16[64,512]{1,0:T(8,128)(2,1)}) custom-call(s32[1]{0:T(128)} %copy.63.lengths, bf16[64,2048]{1,0:T(8,128)(2,1)} %hidden.1, bf16[8,64,128]{2,1,0:T(8,128)(2,1)} %bitcast.30, f32[64,128]{1,0:T(8,128)} %get-tuple-element.11.cosines, f32[64,128]{1,0:T(8,128)} %get-tuple-element.12.sines, ...), custom_call_target="tpu_custom_call" | custom-call | tf_op jit(solution)/shard_map/pallas_call | solution.py:708
  119.8 1.5 %reshape.49 = bf16[64,2,2,128]{3,2,1,0:T(2,128)(2,1)} reshape(bf16[64,512]{1,0:T(8,128)(2,1)} %get-tuple-element.5) | data formatting | bytes 131072 | tf_op jit(solution)/shard_map/reshape | solution.py:808
  121.3 1.7 %copy.64 = bf16[32,4096]{1,0:T(8,128)(2,1)} copy(bf16[32,4096]{1,0:T(8,128)(2,1)} %get-tuple-element.15) | data formatting | bytes 524288
  (10 shorter events, 0.1 us)

commit v3 on v0

v3 whole, which is shorter than its diff:
```python
import functools
import itertools
import math

import jax
import jax.numpy as jnp
from jax import lax
from jax.experimental import pallas as pl
from jax.experimental.pallas import tpu as pltpu
from jax.sharding import PartitionSpec as P

EXPERTS = 4
TOPK = 2
PIECES = 4


eps_norm = 1e-05
rope_base = 1000000.0
mask_fill = -1e30


def rotation(head_dim, positions):
    half_dim = head_dim // 2
    inverse = jnp.exp(
        jnp.arange(half_dim, dtype=jnp.float32) * (-2.0 * math.log(rope_base) / head_dim)
    )
    angle = positions.astype(jnp.float32)[:, None] * inverse[None, :]
    cosine, sine = jnp.cos(angle), jnp.sin(angle)
    return jnp.concatenate([cosine, cosine], axis=1), jnp.concatenate([-sine, sine], axis=1)


def score_rows(query_rows, key_rows, scale_factor):
    return (
        lax.dot_general(
            query_rows, key_rows, (((1,), (1,)), ((), ())), preferred_element_type=jnp.float32
        )
        * scale_factor
    )


MESH = pl.DeviceIdType.MESH
LANES = 128
VMEM = pl.BlockSpec(memory_space=pltpu.VMEM)


def place(tok, mdl):
    return (lax.axis_index("grp"), tok, mdl)


def greet(peers):
    barrier = pltpu.get_barrier_semaphore()
    for peer in peers:
        pl.semaphore_signal(barrier, inc=1, device_id=peer, device_id_type=MESH)
    pl.semaphore_wait(barrier, len(peers))


def peers_of(groups, ranks, cores):
    tok, mdl = lax.axis_index("tok"), lax.axis_index("mdl")
    group, rank = tok // ranks, tok % ranks
    peers = [place((group + d) % groups * ranks + rank, mdl) for d in range(1, groups)]
    peers += [place(group * ranks + (rank + d) % ranks, mdl) for d in range(1, ranks)]
    if cores:
        peers.append(place(tok, 1 - mdl))
    return peers


def remote(src, dst, sems, index, device):
    copy = pltpu.make_async_remote_copy(
        src_ref=src,
        dst_ref=dst,
        send_sem=sems.at[0, index],
        recv_sem=sems.at[1, index],
        device_id=device,
        device_id_type=MESH,
    )
    copy.start()
    return copy


def near_first(count):
    return sorted(range(1, count), key=lambda d: (min(d, count - d), d))


def cut(width, pieces):
    part = width // pieces
    return [pl.ds(c * part, part) for c in range(pieces)]


def divide(width, choices=(256, 128)):
    for part in choices:
        if width % part == 0 and width // part >= 1:
            return part
    return width


def layer_kernel(
    dims,
    lengths,
    hidden,
    flat_queries,
    cosines,
    sines,
    gains,
    expert_ids,
    gates,
    cache_hbm,
    wkv_hbm,
    wo_hbm,
    gate_hbm,
    up_hbm,
    down_hbm,
    mixed,
    fresh,
    full,
    slices,
    own_square,
    other_square,
    part_kv,
    mid_kv,
    sum_kv,
    in_kv,
    heads,
    part_out,
    near_out,
    in_out,
    resid,
    send,
    recv,
    near,
    mid,
    home,
    gate_w,
    up_w,
    down_w,
    picks,
    weights,
    sems,
    load_sems,
):
    groups, ranks, cores, pieces, kv_heads = dims
    tok, mdl = lax.axis_index("tok"), lax.axis_index("mdl")
    group, rank = tok // ranks, tok % ranks
    toks = groups * ranks
    f32, narrow = jnp.float32, jnp.bfloat16

    width = full.shape[1]
    part = width // pieces
    columns = cut(width, pieces)

    def load(index, src, dst):
        return pltpu.make_async_copy(src, dst, load_sems.at[index])

    def load_gate(c):
        return load(4 + c, gate_hbm.at[0, columns[c], :], gate_w.at[columns[c], :])

    def load_up(c):
        return load(4 + pieces + c, up_hbm.at[0, columns[c], :], up_w.at[columns[c], :])

    def load_down(c):
        return load(4 + 2 * pieces + c, down_hbm.at[0, :, columns[c]], down_w.at[c])

    numbers = itertools.count()
    started = []
    other = place(tok, 1 - mdl)
    far = near_first(groups)
    near_ranks = near_first(ranks)
    every_rank = [0] + near_ranks

    def go(src, dst, device):
        copy = remote(src, dst, sems, next(numbers), device)
        started.append(copy)
        return copy

    def all_sent():
        for copy in started:
            copy.wait_send()
        started.clear()

    def rank_place(r):
        return place(group * ranks + (rank + r) % ranks, mdl)

    def group_place(g):
        return place((group + g) % groups * ranks + rank, mdl)

    def group_from(d):
        return (group + groups - d) % groups

    def rank_from(r):
        return (rank + ranks - r) % ranks

    span, features = hidden.shape
    half = span // cores
    depth = width // toks
    head_dim = flat_queries.shape[1]
    query_heads = flat_queries.shape[0] // span
    per_head = query_heads // kv_heads
    query_count = per_head * span
    limit = cache_hbm.shape[0] // (2 * kv_heads)
    main = send.shape[1]
    cap = picks.shape[0] // groups
    total_rows = cores * toks * cap
    hidden_units = gate_w.shape[1]

    def first_part(*scratch):
        attend(*scratch)
        all_sent()

    def second_part(*scratch):
        mix(*scratch)
        all_sent()


    def mixing(kinds, axis):
        per = LANES // kinds
        down = lax.broadcasted_iota(jnp.int32, (LANES, LANES), 1 - axis)
        along = lax.broadcasted_iota(jnp.int32, (LANES, LANES), axis)
        return jnp.where(along == down % per * kinds + down // per, 1.0, 0.0).astype(narrow)

    def put(ref, kind, at, found):
        ref[kind, at, :] = found

    def sort_rows(flat, kinds, store):
        per = LANES // kinds
        gather = mixing(kinds, 1)
        together = 4
        while flat.shape[0] % (together * LANES):
            together -= 1

        def step(n, carry):
            for b in range(together):
                spot = n * together + b
                taken = flat[pl.ds(pl.multiple_of(spot * LANES, LANES), LANES), :]
                found = jnp.dot(gather, taken, preferred_element_type=f32).astype(narrow)
                at = pl.ds(pl.multiple_of(spot * per, per), per)
                for kind in range(kinds):
                    store(kind, at, found[kind * per : (kind + 1) * per])
            return carry

        lax.fori_loop(0, flat.shape[0] // (together * LANES), step, 0)

    def routes():
        slots = -(-groups * cap // LANES) * LANES
        lane = lax.broadcasted_iota(jnp.int32, (half, slots), 1)
        spare = jnp.maximum(lane - groups * main, 0)
        in_main = lane < groups * main
        expert = jnp.where(in_main, lane // main, spare // (cap - main))
        slot = jnp.where(in_main, lane % main, main + spare % (cap - main))
        chosen = jnp.zeros((half, slots), f32)
        share = jnp.zeros((half, slots), f32)
        for k in range(expert_ids.shape[1]):
            match = expert_ids[:, k : k + 1] == expert
            chosen = chosen + jnp.where(match, 1.0, 0.0)
            share = share + jnp.where(match, gates[:, k : k + 1], 0.0)
        later = lax.broadcasted_iota(jnp.int32, (half, half), 0)
        earlier = lax.broadcasted_iota(jnp.int32, (half, half), 1)
        before = jnp.where(earlier < later, 1.0, 0.0).astype(narrow)
        ahead = jnp.dot(before, chosen.astype(narrow), preferred_element_type=f32)
        real = lane < groups * cap
        pick = jnp.where((ahead == slot.astype(f32)) & real, chosen, 0.0)
        picks[...] = pick.T[: groups * cap].astype(narrow)
        left = pick * share
        for k in range(weights.shape[0] // half):
            term = left.astype(narrow)
            weights[k * half : (k + 1) * half, :] = term[:, : groups * cap]
            left = left - term.astype(f32)

    def attend(flat_cache, flat_wkv, queries, cache, wkv, wo, tops, sums, heads_acc):
        wkv_load = load(0, wkv_hbm, flat_wkv)
        cache_load = load(1, cache_hbm, flat_cache)
        wo_load = load(2, wo_hbm, wo)
        wkv_load.start()
        cache_load.start()
        wo_load.start()
        greet(peers_of(toks, 1, True))


        def lines(core):
            return pl.ds(pl.multiple_of(core * half, half), half)

        def half_features(core):
            return pl.ds(pl.multiple_of(core * features, features), features)

        swap = go(hidden.at[lines(1 - mdl), :], full.at[:, half_features(mdl)], other)
        full[:, half_features(mdl)] = hidden[lines(mdl), :]
        values = hidden[...].astype(f32)
        square = jnp.sum(values * values, axis=1, keepdims=True)
        own_square[...] = jnp.broadcast_to(square, own_square.shape)
        swap_square = go(own_square, other_square, other)
        for c in range(pieces):
            load_gate(c).start()
            load_up(c).start()
        for c in range(pieces):
            load_down(c).start()
        swap.wait_recv()

        def slice_of(target):
            return pl.ds(pl.multiple_of(target * depth, depth), depth)

        outward, twin = {}, {}
        for d in [0] + far:
            for r in every_rank:
                target = (group + d) % groups * ranks + (rank + r) % ranks
                if d or r:
                    outward[d, r] = go(
                        full.at[:, slice_of(target)],
                        slices.at[group, rank, mdl],
                        place(target, mdl),
                    )
        slices[group, rank, mdl] = full[:, slice_of(tok)]
        twin[0, 0] = go(full.at[:, slice_of(tok)], slices.at[group, rank, mdl], other)

        scale_factor = 1.0 / math.sqrt(head_dim)
        block = min(512, limit)

        def query_rows(h):
            return queries[h * per_head : (h + 1) * per_head].reshape(query_count, head_dim)

        def cached_attention(h):
            asked = query_rows(h)
            scores, values = [], []
            for start in range(0, limit, block):
                position = lax.broadcasted_iota(jnp.int32, (query_count, block), 1) + start
                score = score_rows(asked, cache[h, 0, pl.ds(start, block)], scale_factor)
                scores.append(jnp.where(position < lengths[0], score, mask_fill))
                values.append(cache[h, 1, pl.ds(start, block)])
            top = functools.reduce(jnp.maximum, [jnp.max(x, axis=1, keepdims=True) for x in scores])
            total = jnp.zeros((query_count, 1), f32)
            found_values = jnp.zeros((query_count, head_dim), f32)
            for score, value_rows in zip(scores, values):
                chance = jnp.exp(score - top)
                total += jnp.sum(chance, axis=1, keepdims=True)
                found_values += jnp.dot(chance.astype(narrow), value_rows, preferred_element_type=f32)
            tops[h] = jnp.broadcast_to(top, (query_count, head_dim))
            sums[h] = jnp.broadcast_to(total, (query_count, head_dim))
            heads_acc[h] = found_values

        sort_rows(flat_queries, query_heads, lambda kind, at, found: put(queries, kind, at, found))
        cache_load.wait()
        sort_rows(
            flat_cache,
            2 * kv_heads,
            lambda kind, at, found: put(cache.at[kind // 2], kind % 2, at, found),
        )
        wkv_load.wait()

        def put_wkv(kind, at, found):
            wkv[at, kind * head_dim : (kind + 1) * head_dim] = found

        sort_rows(flat_wkv, 2 * kv_heads, put_wkv)
        routes()
        cached_attention(0)

        kv_width = wkv.shape[1]
        gain_rows = depth // LANES
        gain_slice = jnp.concatenate(
            [gains[pl.ds(tok * gain_rows + b, 1), :] for b in range(gain_rows)], axis=1
        )
        kv_rank, kv_home = {}, {}

        def project_kv(d):
            source = group_from(d)
            for r in every_rank:
                if d or r:
                    outward[d, r].wait_recv()
                    landed = slices.at[source, rank_from(r), mdl]
                    twin[d, r] = go(landed, landed, other)
            for r in every_rank:
                twin[d, r].wait_recv()
            taken = slices[source].reshape(ranks * span, depth).astype(f32) * gain_slice
            part_kv[source] = (
                jnp.dot(taken.astype(narrow), wkv[...], preferred_element_type=f32)
                .astype(narrow)
                .reshape(ranks, span, kv_width)
            )
            for r in near_ranks:
                kv_rank[d, r] = go(
                    part_kv.at[source, (rank + r) % ranks], mid_kv.at[r - 1, source], rank_place(r)
                )

        def reduce_kv(d):
            source = group_from(d)
            total = part_kv[source, rank].astype(f32)
            for r in near_ranks:
                kv_rank[d, r].wait_recv()
                total = total + mid_kv[r - 1, source].astype(f32)
            if d:
                sum_kv[source] = total.astype(narrow)
                kv_home[d] = go(sum_kv.at[source], in_kv.at[group], group_place(-d))
            else:
                in_kv[group] = total.astype(narrow)

        order = [0] + far
        for s in range(groups + 1):
            if s < groups:
                project_kv(order[s])
            if s > 0:
                reduce_kv(order[s - 1])
        for h in range(1, kv_heads):
            cached_attention(h)
        swap_square.wait_recv()
        meansq = (own_square[...] + other_square[...]) * (1.0 / width)
        row_scale = lax.rsqrt(meansq + eps_norm)
        for d in far:
            kv_home[d].wait_recv()

        token = lax.broadcasted_iota(jnp.int32, (query_count, span), 0) % span
        column = lax.broadcasted_iota(jnp.int32, (query_count, span), 1)
        head_width = per_head * head_dim
        head_columns = [pl.ds(h * head_width, head_width) for h in range(kv_heads)]
        head_group, head_rank = {}, {}
        new_rows = []
        for h in range(kv_heads):
            pair_of = []
            for kind in range(2):
                at = pl.ds((2 * h + kind) * head_dim, head_dim)
                total = in_kv[0, :, at].astype(f32)
                for g in range(1, groups):
                    total = total + in_kv[g, :, at].astype(f32)
                total = total * row_scale
                if kind == 0:
                    total = total * cosines[...] + pltpu.roll(total, head_dim // 2, 1) * sines[...]
                pair_of.append(total.astype(narrow))
                new_rows.append(pair_of[kind])
            score = score_rows(query_rows(h), pair_of[0], scale_factor)
            score = jnp.where(column <= token, score, mask_fill)
            before = tops[h]
            top = jnp.maximum(before, jnp.max(score, axis=1, keepdims=True))
            fade = jnp.exp(before - top)
            chance = jnp.exp(score - top[:, :1])
            total = sums[h] * fade + jnp.sum(chance, axis=1, keepdims=True)
            attended = heads_acc[h] * fade + jnp.dot(
                chance.astype(narrow), pair_of[1], preferred_element_type=f32
            )
            attended = (attended / total).astype(narrow)
            for head in range(per_head):
                at = pl.ds(h * head_width + head * head_dim, head_dim)
                heads[group, rank, :, at] = attended[head * span : (head + 1) * span]
            own = heads.at[group, rank, :, head_columns[h]]
            for d in far:
                head_group[h, d] = go(own, own, group_place(d))
            for r in near_ranks:
                head_rank[h, 0, r] = go(own, own, rank_place(r))

        kinds = 2 * kv_heads
        step_rows = LANES // kinds
        spread_out = mixing(kinds, 0)
        for b in range(span // step_rows):
            stack = jnp.concatenate(
                [x[b * step_rows : (b + 1) * step_rows] for x in new_rows], axis=0
            )
            fresh[b * LANES : (b + 1) * LANES, :] = jnp.dot(
                spread_out, stack, preferred_element_type=f32
            ).astype(narrow)
        out_width = wo.shape[1]
        wo_load.wait()
        out_core, out_home = {}, {}

        def forward_heads(d):
            for h in range(kv_heads):
                head_group[h, d].wait_recv()
                landed = heads.at[group_from(d), rank, :, head_columns[h]]
                for r in near_ranks:
                    head_rank[h, d, r] = go(landed, landed, rank_place(r))

        def project_out(d):
            source = group_from(d)
            for h in range(kv_heads):
                for r in near_ranks:
                    head_rank[h, d, r].wait_recv()
            part_out[source] = (
                jnp.dot(
                    heads[source].reshape(ranks * span, heads.shape[3]),
                    wo[...],
                    preferred_element_type=f32,
                )
                .astype(narrow)
                .reshape(ranks, cores, half, out_width)
            )
            out_core[d] = go(part_out.at[source, :, 1 - mdl], near_out.at[source], other)

        def send_out(d):
            source = group_from(d)
            out_core[d].wait_recv()
            for r in every_rank:
                giver = rank_from(r)
                total = part_out[source, giver, mdl].astype(f32) + near_out[source, giver].astype(f32)
                if d or r:
                    part_out[source, giver, mdl] = total.astype(narrow)
                    out_home[d, r] = go(
                        part_out.at[source, giver, mdl],
                        in_out.at[tok],
                        place(source * ranks + giver, mdl),
                    )
                else:
                    in_out[tok] = total.astype(narrow)

        for s in range(groups + 2):
            if 0 < s < groups:
                forward_heads(order[s])
            if 0 <= s - 1 < groups:
                project_out(order[s - 1])
            if 0 <= s - 2 < groups:
                send_out(order[s - 2])
        for d in order:
            for r in every_rank:
                if d or r:
                    out_home[d, r].wait_recv()
        square = jnp.zeros((half, 1), f32)
        for t in range(toks):
            at = pl.ds(t * depth, depth)
            total = full[:, at].astype(f32) + in_out[t].astype(f32)
            resid[:, at] = total
            square += jnp.sum(total * total, axis=1, keepdims=True)
        row_scale = lax.rsqrt(square * (1.0 / width) + eps_norm)
        all_sent()
        for b in range(width // LANES):
            at = pl.ds(b * LANES, LANES)
            gain = gains[width // LANES + b : width // LANES + b + 1, :]
            full[:, at] = (resid[:, at] * row_scale * gain).astype(narrow)

    def mix(rows, gate_acc, up_acc, slab):
        tokens = full
        rest = cap - main
        packed = cut(send.shape[2], pieces)
        blocks = part // LANES
        main_rows = cores * toks * main
        tile = divide(hidden_units)

        def pack(target, lead, rows_in, row, c):
            for b in range(blocks):
                spot, lane = divmod(b, main // rest)
                at = c * (send.shape[2] // pieces) + part + spot * LANES
                target[(*lead, pl.ds(lane * rest, rest), pl.ds(at, LANES))] = rows_in[
                    row : row + rest, b * LANES : (b + 1) * LANES
                ]

        def unpack(target, row, source, lead, c):
            for b in range(blocks):
                spot, lane = divmod(b, main // rest)
                at = c * (send.shape[2] // pieces) + part + spot * LANES
                target[row : row + rest, b * LANES : (b + 1) * LANES] = source[
                    (*lead, pl.ds(lane * rest, rest), pl.ds(at, LANES))
                ]

        def body(c):
            return pl.ds(c * (send.shape[2] // pieces), part)

        by_group, by_rank, by_core = {}, {}, {}
        for c in range(pieces):
            picked = jnp.dot(
                picks[...], tokens[:, columns[c]], preferred_element_type=jnp.float32
            ).astype(send.dtype)
            for e in range(groups):
                send[e, :, body(c)] = picked[e * main : (e + 1) * main]
                pack(send, (e,), picked, groups * main + e * rest, c)
            for d in far:
                by_group[c, d] = go(
                    send.at[(group + d) % groups, :, packed[c]],
                    recv.at[mdl, group, rank, :, packed[c]],
                    group_place(d),
                )
            for r in near_ranks:
                by_rank[c, 0, r] = go(
                    send.at[group, :, packed[c]],
                    recv.at[mdl, group, rank, :, packed[c]],
                    rank_place(r),
                )
            by_core[c, 0, 0] = go(
                send.at[group, :, packed[c]], recv.at[mdl, group, rank, :, packed[c]], other
            )

        recv[mdl, group, rank] = send[group]

        def from_groups(c):
            for d in far:
                by_group[c, d].wait_recv()
                source = (group + groups - d) % groups
                block = recv.at[mdl, source, rank, :, packed[c]]
                for r in near_ranks:
                    by_rank[c, d, r] = go(block, block, rank_place(r))
                by_core[c, d, 0] = go(block, block, other)

        def from_ranks(c):
            for d in [0] + far:
                for r in near_ranks:
                    by_rank[c, d, r].wait_recv()
                    source = (group + groups - d) % groups
                    giver = (rank + ranks - r) % ranks
                    block = recv.at[mdl, source, giver, :, packed[c]]
                    by_core[c, d, r] = go(block, block, other)

        def assemble(c):
            for d in [0] + far:
                for r in [0] + near_ranks:
                    by_core[c, d, r].wait_recv()
            rows[0:main_rows, :] = recv[:, :, :, :, body(c)].reshape(main_rows, part)
            spot = main_rows
            for m in range(cores):
                for g in range(groups):
                    for r in range(ranks):
                        unpack(rows, spot, recv, (m, g, r), c)
                        spot += rest

        def project(c):
            assemble(c)
            load_gate(c).wait()
            load_up(c).wait()

            def step(n, carry):
                at = pl.ds(pl.multiple_of(n * tile, tile), tile)
                x = rows[...]
                gate_val = jnp.dot(x, gate_w[columns[c], at], preferred_element_type=jnp.float32)
                up_val = jnp.dot(x, up_w[columns[c], at], preferred_element_type=jnp.float32)
                if c > 0:
                    gate_val = gate_val + gate_acc[:, at]
                    up_val = up_val + up_acc[:, at]
                if c < pieces - 1:
                    gate_acc[:, at] = gate_val
                    up_acc[:, at] = up_val
                else:
                    slab[:, at] = (gate_val / (1.0 + jnp.exp(-gate_val)) * up_val).astype(slab.dtype)
                return carry

            lax.fori_loop(0, hidden_units // tile, step, 0)

        for s in range(pieces + 2):
            if s < pieces:
                from_groups(s)
            if 0 <= s - 1 < pieces:
                from_ranks(s - 1)
            if 0 <= s - 2 < pieces:
                project(s - 2)

        all_sent()
        down_tile = divide(part)
        across, to_rank, to_home = {}, {}, {}

        def down(c):
            load_down(c).wait()

            def step(n, carry):
                at = pl.multiple_of(n * down_tile, down_tile)
                rows[:, pl.ds(at, down_tile)] = jnp.dot(
                    slab[...],
                    down_w[c, :, pl.ds(at, down_tile)],
                    preferred_element_type=jnp.float32,
                ).astype(rows.dtype)
                return carry

            lax.fori_loop(0, part // down_tile, step, 0)
            recv[:, :, :, :, body(c)] = rows[0:main_rows, :].reshape(cores, groups, ranks, main, part)
            spot = main_rows
            for m in range(cores):
                for g in range(groups):
                    for r in range(ranks):
                        pack(recv, (m, g, r), rows, spot, c)
                        spot += rest
            across[c] = go(
                recv.at[1 - mdl, :, :, :, packed[c]], near.at[:, :, :, packed[c]], other
            )

        def pair(g, r, c):
            return recv[mdl, g, r, :, packed[c]].astype(jnp.float32) + near[
                g, r, :, packed[c]
            ].astype(jnp.float32)

        def to_ranks(c):
            across[c].wait_recv()
            for r in near_ranks:
                there = (rank + r) % ranks
                for g in range(groups):
                    recv[mdl, g, there, :, packed[c]] = pair(g, there, c).astype(recv.dtype)
                to_rank[c, r] = go(
                    recv.at[mdl, :, there, :, packed[c]], mid.at[r - 1, :, :, packed[c]], rank_place(r)
                )

        def to_sources(c):
            for r in near_ranks:
                to_rank[c, r].wait_recv()
            for d in far[::-1] + [0]:
                there = (group + d) % groups
                total = pair(there, rank, c)
                for r in near_ranks:
                    total = total + mid[r - 1, there, :, packed[c]].astype(jnp.float32)
                if d == 0:
                    home[group, :, packed[c]] = total.astype(home.dtype)
                else:
                    recv[mdl, there, rank, :, packed[c]] = total.astype(recv.dtype)
                    to_home[c, d] = go(
                        recv.at[mdl, there, rank, :, packed[c]],
                        home.at[group, :, packed[c]],
                        group_place(d),
                    )

        def finish(c):
            for d in far:
                to_home[c, d].wait_recv()
            rows[0 : groups * main, :] = home[:, :, body(c)].reshape(groups * main, part)
            for e in range(groups):
                unpack(rows, groups * main + e * rest, home, (e,), c)
            terms = jnp.dot(
                weights[...], rows[0 : groups * cap, :], preferred_element_type=jnp.float32
            )
            total = resid[:, columns[c]]
            for k in range(weights.shape[0] // resid.shape[0]):
                total = total + terms[k * resid.shape[0] : (k + 1) * resid.shape[0]]
            mixed[:, columns[c]] = total.astype(mixed.dtype)

        lag_rank, lag_source, lag_end = 1, 2, 4
        for s in range(pieces + lag_end):
            if s < pieces:
                down(s)
            if 0 <= s - lag_rank < pieces:
                to_ranks(s - lag_rank)
            if 0 <= s - lag_source < pieces:
                to_sources(s - lag_source)
            if 0 <= s - lag_end < pieces:
                finish(s - lag_end)

    scoped = [
        (cache_hbm.shape, narrow),
        (wkv_hbm.shape, narrow),
        ((query_heads, span, head_dim), narrow),
        ((kv_heads, 2, limit, head_dim), narrow),
        ((depth, 2 * kv_heads * head_dim), narrow),
        (wo_hbm.shape, narrow),
        ((kv_heads, query_count, head_dim), f32),
        ((kv_heads, query_count, head_dim), f32),
        ((kv_heads, query_count, head_dim), f32),
    ]
    pl.run_scoped(first_part, *[pltpu.VMEM(shape, kind) for shape, kind in scoped])
    scoped = [
        ((total_rows, part), narrow),
        ((total_rows, hidden_units), f32),
        ((total_rows, hidden_units), f32),
        ((total_rows, hidden_units), narrow),
    ]
    pl.run_scoped(second_part, *[pltpu.VMEM(shape, kind) for shape, kind in scoped])


def layer(
    dims,
    lengths,
    hidden,
    queries,
    cosines,
    sines,
    gains,
    expert_ids,
    gates,
    cache,
    wkv,
    wo,
    w_gate,
    w_up,
    w_down,
):
    groups, ranks, cores, pieces, kv_heads = dims
    toks = groups * ranks
    span, features = hidden.shape
    half, width = span // cores, features * cores
    cap = half * TOPK * 9 // (8 * groups)
    main = cap // 16 * 16
    packed = width // main * cap
    depth, units = w_gate.shape[1:]
    part = width // pieces
    head_dim = queries.shape[1]
    kv_width, out_width = 2 * kv_heads * head_dim, wo.shape[1]
    depth_slice = width // toks
    dtype, f32 = hidden.dtype, jnp.float32
    more = max(ranks - 1, 1)
    copies = (
        2
        + (2 * toks - 1)
        + groups * (ranks - 1)
        + groups
        - 1
        + kv_heads * (groups - 1 + groups * (ranks - 1))
        + groups
        + toks
        - 1
        + pieces * ((groups - 1) * 2 + (groups + 1) * (ranks - 1) + toks + 1)
    )
    remote_space = pl.BlockSpec(memory_space=pl.ANY)
    buffers = [
        ((half, width), dtype),
        ((groups, ranks, cores, half, depth_slice), dtype),
        ((span, head_dim), f32),
        ((span, head_dim), f32),
        ((groups, ranks, span, kv_width), dtype),
        ((more, groups, span, kv_width), dtype),
        ((groups, span, kv_width), dtype),
        ((groups, span, kv_width), dtype),
        ((groups, ranks, span, wo.shape[0]), dtype),
        ((groups, ranks, cores, half, out_width), dtype),
        ((groups, ranks, half, out_width), dtype),
        ((toks, half, out_width), dtype),
        ((half, width), f32),
        ((groups, main, packed), dtype),
        ((cores, groups, ranks, main, packed), dtype),
        ((groups, ranks, main, packed), dtype),
        ((more, groups, main, packed), dtype),
        ((groups, main, packed), dtype),
        ((depth, units), dtype),
        ((depth, units), dtype),
        ((pieces, units, part), dtype),
        ((groups * cap, half), dtype),
        ((3 * half, groups * cap), dtype),
    ]
    return pl.pallas_call(
        functools.partial(layer_kernel, dims),
        out_shape=(
            jax.ShapeDtypeStruct((half, width), dtype),
            jax.ShapeDtypeStruct((span * 2 * kv_heads, head_dim), dtype),
        ),
        in_specs=[pl.BlockSpec(memory_space=pltpu.SMEM)] + [VMEM] * 7 + [remote_space] * 6,
        out_specs=(VMEM, VMEM),
        scratch_shapes=[pltpu.VMEM(shape, kind) for shape, kind in buffers]
        + [
            pltpu.SemaphoreType.DMA((2, copies)),
            pltpu.SemaphoreType.DMA((3 * pieces + 4,)),
        ],
        compiler_params=pltpu.CompilerParams(
            collective_id=1, has_side_effects=True, vmem_limit_bytes=67043328
        ),
    )(
        lengths,
        hidden,
        queries,
        cosines,
        sines,
        gains,
        expert_ids,
        gates,
        cache,
        wkv,
        wo,
        w_gate,
        w_up,
        w_down,
    )


def shards(
    hidden,
    queries,
    cache,
    cache_lengths,
    wkv,
    wo,
    attn_gain,
    moe_gain,
    w_gate,
    w_up,
    w_down,
    expert_ids,
    gates,
):
    span_len = hidden.shape[0]
    toks = lax.axis_size("tok")
    core_count = lax.axis_size("mdl")
    ranks = toks // EXPERTS
    kv_heads, _, head_dim = wkv.shape[1:]
    positions = cache_lengths[0] + jnp.arange(span_len, dtype=jnp.int32)
    cosines, sines = rotation(head_dim, positions)
    gains = jnp.concatenate([attn_gain, moe_gain]).astype(jnp.float32).reshape(-1, LANES)
    mixed, fresh = layer(
        (EXPERTS, ranks, core_count, PIECES, kv_heads),
        cache_lengths,
        hidden,
        queries.reshape(-1, head_dim),
        cosines,
        sines,
        gains,
        expert_ids,
        gates,
        cache.reshape(-1, head_dim),
        wkv.reshape(-1, head_dim),
        wo.reshape(-1, wo.shape[2]),
        w_gate,
        w_up,
        w_down,
    )
    fresh_key_value = fresh.reshape(span_len, kv_heads, 2, head_dim)
    return (mixed, fresh_key_value)


def solution(mesh):
    in_specs = (
        P(("grp", "tok"), "mdl"),
        P(("grp", "tok"), "mdl", None),
        P(("grp", "tok"), None, "mdl", None, None),
        P(("grp", "tok")),
        P("tok", "mdl", None, None),
        P("mdl", None, "tok"),
        P(),
        P(),
        P(("tok", "mdl"), None, None),
        P(("tok", "mdl"), None, None),
        P(("tok", "mdl"), None, None),
        P(("grp", "tok", "mdl"), None),
        P(("grp", "tok", "mdl"), None),
    )
    out_specs = (P(("grp", "tok", "mdl"), None), P(("grp", "tok"), "mdl", None, None))
    return jax.shard_map(shards, mesh=mesh, in_specs=in_specs, out_specs=out_specs, check_vma=False)
```

time: 157 us -> 116 us (0.74)
  matrix products: 26.6 us -> 0 us
  Pallas kernels: 114 us -> 107 us
  local copies, waits for them, and re-layouts: 10.2 us -> 5.9 us
  blocking collectives: 2.64 us -> 0 us
    dot_general x7 -> x0, matrix products: 26.6 us -> none  [the longest x1 9.85 us: shards(): up_val = jnp.dot(flat_rows, w_up[0], preferred_element_type=jnp.float32)]
    pallas_call x7 -> x1, Pallas kernels: 114 us -> 107 us  [layer(): pl.pallas_call(functools.partial(layer_kernel, dims), out_shape=(jax.Shap...]
    reshape x5 -> x0, local copies, waits for them, and re-layouts: 5.01 us -> none  [the longest x1 2.44 us: shards(): slab_out.reshape(received.shape)]
    all_gather x1 -> x0, blocking collectives: 2.64 us -> none  [shards(): full_rows = lax.all_gather(hidden, 'mdl', axis=1, tiled=True)]
    unnamed x39 -> x4, local copies, waits for them, and re-layouts: 4.86 us -> 5.9 us
where the time goes in v3:
time: 116 us
  Pallas kernels  107 us (92%)
  local copies, waits for them, and re-layouts  5.9 us (5%)
  other arithmetic  2.25 us (2%)
  between operations  1.3 us (1%)
    pallas_call x1, Pallas kernels, layer(): pl.pallas_call(functools.partial(layer_kernel, dims), out_shape=(jax.Shap...  107 us
    unnamed x4, local copies, waits for them, and re-layouts  5.9 us

profile of v3, /device:TPU:0, one launch (start us, length us, event | category | flops | bytes accessed | tf_op | source)
XLA Modules:
  0.0 116.1 jit_solution(935745483404927081)
XLA Ops:
  1.3 1.4 %copy.15.expert_ids = s32[32,2]{1,0:T(8,128)} copy(s32[32,2]{0,1:T(2,128)} %param.24) | data formatting | bytes 512 | tf_op args[11]
  2.7 1.4 %copy.16.gates = f32[32,2]{1,0:T(8,128)} copy(f32[32,2]{0,1:T(2,128)} %param.25) | data formatting | bytes 512 | tf_op args[12]
  4.0 1.3 %maximum_convert_fusion.gains = f32[64,128]{1,0:T(8,128)} fusion(bf16[32,128]{1,0:T(8,128)(2,1)} %bitcast.14, bf16[32,128]{1,0:T(8,128)(2,1)} %bitcast.15), kind=kLoop, calls=%fused_computation.4 | loop fusion | flops 32768 | bytes 49152 | tf_op jit(solution)/shard_map/convert_element_type | solution.py:866
  5.3 0.2 fusion
  5.5 0.7 pad_maximum_fusion
  6.3 106.6 %shard_map.140 = (bf16[32,4096]{1,0:T(8,128)(2,1)}, bf16[256,128]{1,0:T(8,128)(2,1)}) custom-call(s32[1]{0:T(128)} %copy.19.lengths, bf16[64,2048]{1,0:T(8,128)(2,1)} %hidden.1, bf16[512,128]{1,0:T(8,128)(2,1)} %bitcast.12, f32[64,128]{1,0:T(8,128)} %get-tuple-element.9.cosines, f32[64,128]{1,0:T(8,128)} %get-tuple-element.10.sines, ...), custom_call_target="tpu_custom_call" | custom-call | tf_op jit(solution)/shard_map/pallas_call | solution.py:810
  112.9 1.7 %copy.20 = bf16[32,4096]{1,0:T(8,128)(2,1)} copy(bf16[32,4096]{1,0:T(8,128)(2,1)} %get-tuple-element.13) | data formatting | bytes 524288
  114.6 1.5 %copy.21 = bf16[64,2,2,128]{3,2,1,0:T(2,128)(2,1)} copy(bf16[64,2,2,128]{3,2,1,0:T(2,128)(2,1)} %bitcast.13) | data formatting | bytes 131072
  (2 shorter events, 0.0 us)

commit v4 on v3

--- a/solution.py
+++ b/solution.py
@@ -26,7 +26,7 @@
     )
     angle = positions.astype(jnp.float32)[:, None] * inverse[None, :]
     cosine, sine = jnp.cos(angle), jnp.sin(angle)
-    return jnp.concatenate([cosine, cosine], axis=1), jnp.concatenate([-sine, sine], axis=1)
+    return cosine, sine
 
 
 def score_rows(query_rows, key_rows, scale_factor):
@@ -101,8 +101,6 @@
     cosines,
     sines,
     gains,
-    expert_ids,
-    gates,
     cache_hbm,
     wkv_hbm,
     wo_hbm,
@@ -247,10 +245,11 @@
         slot = jnp.where(in_main, lane % main, main + spare % (cap - main))
         chosen = jnp.zeros((half, slots), f32)
         share = jnp.zeros((half, slots), f32)
-        for k in range(expert_ids.shape[1]):
-            match = expert_ids[:, k : k + 1] == expert
+        named = gains[gains.shape[0] - half :, :]
+        for k in range(TOPK):
+            match = named[:, k : k + 1] == expert.astype(f32)
             chosen = chosen + jnp.where(match, 1.0, 0.0)
-            share = share + jnp.where(match, gates[:, k : k + 1], 0.0)
+            share = share + jnp.where(match, named[:, TOPK + k : TOPK + k + 1], 0.0)
         later = lax.broadcasted_iota(jnp.int32, (half, half), 0)
         earlier = lax.broadcasted_iota(jnp.int32, (half, half), 1)
         before = jnp.where(earlier < later, 1.0, 0.0).astype(narrow)
@@ -347,8 +346,6 @@
             wkv[at, kind * head_dim : (kind + 1) * head_dim] = found
 
         sort_rows(flat_wkv, 2 * kv_heads, put_wkv)
-        routes()
-        cached_attention(0)
 
         kv_width = wkv.shape[1]
         gain_rows = depth // LANES
@@ -395,7 +392,7 @@
                 project_kv(order[s])
             if s > 0:
                 reduce_kv(order[s - 1])
-        for h in range(1, kv_heads):
+        for h in range(kv_heads):
             cached_attention(h)
         swap_square.wait_recv()
         meansq = (own_square[...] + other_square[...]) * (1.0 / width)
@@ -407,6 +404,8 @@
         column = lax.broadcasted_iota(jnp.int32, (query_count, span), 1)
         head_width = per_head * head_dim
         head_columns = [pl.ds(h * head_width, head_width) for h in range(kv_heads)]
+        turn = jnp.concatenate([cosines[...], cosines[...]], axis=1)
+        shift = jnp.concatenate([-sines[...], sines[...]], axis=1)
         head_group, head_rank = {}, {}
         new_rows = []
         for h in range(kv_heads):
@@ -418,7 +417,7 @@
                     total = total + in_kv[g, :, at].astype(f32)
                 total = total * row_scale
                 if kind == 0:
-                    total = total * cosines[...] + pltpu.roll(total, head_dim // 2, 1) * sines[...]
+                    total = total * turn + pltpu.roll(total, head_dim // 2, 1) * shift
                 pair_of.append(total.astype(narrow))
                 new_rows.append(pair_of[kind])
             score = score_rows(query_rows(h), pair_of[0], scale_factor)
@@ -453,6 +452,7 @@
             ).astype(narrow)
         out_width = wo.shape[1]
         wo_load.wait()
+        routes()
         out_core, out_home = {}, {}
 
         def forward_heads(d):
@@ -746,8 +746,6 @@
     cosines,
     sines,
     gains,
-    expert_ids,
-    gates,
     cache,
     wkv,
     wo,
@@ -813,7 +811,7 @@
             jax.ShapeDtypeStruct((half, width), dtype),
             jax.ShapeDtypeStruct((span * 2 * kv_heads, head_dim), dtype),
         ),
-        in_specs=[pl.BlockSpec(memory_space=pltpu.SMEM)] + [VMEM] * 7 + [remote_space] * 6,
+        in_specs=[pl.BlockSpec(memory_space=pltpu.SMEM)] + [VMEM] * 5 + [remote_space] * 6,
         out_specs=(VMEM, VMEM),
         scratch_shapes=[pltpu.VMEM(shape, kind) for shape, kind in buffers]
         + [
@@ -830,8 +828,6 @@
         cosines,
         sines,
         gains,
-        expert_ids,
-        gates,
         cache,
         wkv,
         wo,
@@ -863,7 +859,13 @@
     kv_heads, _, head_dim = wkv.shape[1:]
     positions = cache_lengths[0] + jnp.arange(span_len, dtype=jnp.int32)
     cosines, sines = rotation(head_dim, positions)
-    gains = jnp.concatenate([attn_gain, moe_gain]).astype(jnp.float32).reshape(-1, LANES)
+    named = jnp.concatenate([expert_ids.astype(jnp.float32), gates], axis=1)
+    gains = jnp.concatenate(
+        [
+            jnp.concatenate([attn_gain, moe_gain]).astype(jnp.float32).reshape(-1, LANES),
+            jnp.pad(named, ((0, 0), (0, LANES - named.shape[1]))),
+        ]
+    )
     mixed, fresh = layer(
         (EXPERTS, ranks, core_count, PIECES, kv_heads),
         cache_lengths,
@@ -872,8 +874,6 @@
         cosines,
         sines,
         gains,
-        expert_ids,
-        gates,
         cache.reshape(-1, head_dim),
         wkv.reshape(-1, head_dim),
         wo.reshape(-1, wo.shape[2]),

time: 116 us -> 114 us (0.983)
  local copies, waits for them, and re-layouts: 5.9 us -> 3.27 us
  Pallas kernels: 107 us -> 105 us
  other arithmetic: 2.25 us -> 3.54 us
    unnamed x4 -> x2, local copies, waits for them, and re-layouts: 5.9 us -> 3.18 us
    pallas_call x1, Pallas kernels: 107 us -> 105 us  [layer(): pl.pallas_call(functools.partial(layer_kernel, dims), out_shape=(jax.Shap...]
where the time goes in v4:
time: 114 us; the launch traced here: 113 us
  Pallas kernels  105 us (92%)
  other arithmetic  3.54 us (3%)
  local copies, waits for them, and re-layouts  3.27 us (3%)
  between operations  1.3 us (1%)
    pallas_call x1, Pallas kernels, layer(): pl.pallas_call(functools.partial(layer_kernel, dims), out_shape=(jax.Shap...  105 us
    unnamed x2, local copies, waits for them, and re-layouts  3.18 us

profile of v4, /device:TPU:0, one launch (start us, length us, event | category | flops | bytes accessed | tf_op | source)
XLA Modules:
  0.0 113.3 jit_solution(7444676651499799090)
XLA Ops:
  1.3 0.7 convert_element_type.18
  2.0 0.7 pad_maximum_fusion
  2.7 0.1 copy.17
  2.8 0.7 maximum_convert_fusion
  3.5 0.6 select_maximum_fusion.gains
  4.1 0.8 multiply_sine_fusion
  4.9 105.2 %shard_map.140 = (bf16[32,4096]{1,0:T(8,128)(2,1)}, bf16[256,128]{1,0:T(8,128)(2,1)}) custom-call(s32[1]{0:T(128)} %copy.20.lengths, bf16[64,2048]{1,0:T(8,128)(2,1)} %hidden.1, bf16[512,128]{1,0:T(8,128)(2,1)} %bitcast.12, f32[64,64]{1,0:T(8,128)} %get-tuple-element.7.cosines, f32[64,64]{1,0:T(8,128)} %get-tuple-element.6.sines, ...), custom_call_target="tpu_custom_call" | custom-call | tf_op jit(solution)/shard_map/pallas_call | solution.py:808
  110.2 1.7 %copy.21 = bf16[32,4096]{1,0:T(8,128)(2,1)} copy(bf16[32,4096]{1,0:T(8,128)(2,1)} %get-tuple-element.10) | data formatting | bytes 524288
  111.8 1.5 %copy.22 = bf16[64,2,2,128]{3,2,1,0:T(2,128)(2,1)} copy(bf16[64,2,2,128]{3,2,1,0:T(2,128)(2,1)} %bitcast.13) | data formatting | bytes 131072
  (2 shorter events, 0.0 us)
